TPU v7x, 8 devices: a whole 2x2x1 slice. The times are simulated.
8 devices in a mesh: dp: 1 (over z), fsdp: 8 (over y, x, core).
Axes of the slice: x: 2, y: 2, z: 1, core: 2. Of those that a mesh axis runs over, the one named last changes fastest.
Arguments:
- hidden_in: bfloat16 [8, 192, 2048], P(('dp', 'fsdp'))
- lengths: int32 [8], P(('dp', 'fsdp'))
- ln_attn_g: float32 [2, 2048], P(None, 'fsdp')
- ln_attn_b: float32 [2, 2048], P(None, 'fsdp')
- ln_mlp_g: float32 [2, 2048], P(None, 'fsdp')
- ln_mlp_b: float32 [2, 2048], P(None, 'fsdp')
- w_qkv: bfloat16 [2, 2048, 4, 4, 256], P(None, 'fsdp')
- w_out: bfloat16 [2, 2048, 2048], P(None, 'fsdp')
- w_up: bfloat16 [2, 2048, 8192], P(None, 'fsdp')
- w_down: bfloat16 [2, 8192, 2048], P(None, 'fsdp')
Outputs:
- output 1: bfloat16 [8, 192, 2048], P(('dp', 'fsdp'))
- output 2: bfloat16 [2, 8, 4, 192, 256], P(None, ('dp', 'fsdp'))
- output 3: bfloat16 [2, 8, 4, 192, 256], P(None, ('dp', 'fsdp'))
All inputs are finite; a program needn't handle non-finite values.
Results may differ from a plain program's by a relative error of at most 0.0100703.
Values are sent between devices in bfloat16 or wider.
A program may use at most 1 GiB of HBM per device.

v0:
```python
import jax
import jax.numpy as jnp
from jax import lax
from jax.sharding import PartitionSpec as P

LN_EPS = 1e-5
ROPE_BASE = 10000.0


def layer_norm(hidden, gain_vec, bias_vec):
    hidden_f = hidden.astype(jnp.float32)
    row_mean = jnp.mean(hidden_f, axis=-1, keepdims=True)
    centered = hidden_f - row_mean
    variance = jnp.mean(centered * centered, axis=-1, keepdims=True)
    return (centered * lax.rsqrt(variance + LN_EPS) * gain_vec + bias_vec).astype(jnp.bfloat16)


def rope_tables(seq_len, head_dim):
    half_dim = head_dim // 2
    inv_freq = ROPE_BASE ** (-2.0 * jnp.arange(half_dim, dtype=jnp.float32) / head_dim)
    angles = jnp.arange(seq_len, dtype=jnp.float32)[:, None] * inv_freq[None, :]
    cos_half = jnp.cos(angles)
    sin_half = jnp.sin(angles)
    return jnp.concatenate([cos_half, cos_half], axis=-1), jnp.concatenate([sin_half, sin_half], axis=-1)


def rotary(values, cos_full, sin_full):
    vals_f = values.astype(jnp.float32)
    half_dim = vals_f.shape[-1] // 2
    rotated = jnp.concatenate([-vals_f[..., half_dim:], vals_f[..., :half_dim]], axis=-1)
    return (vals_f * cos_full + rotated * sin_full).astype(jnp.bfloat16)


def attend_one(seq_item):
    queries, key_rot, values, length = seq_item
    seq_len = queries.shape[0]
    scores = jnp.einsum("qkgh,skh->kgqs", queries, key_rot, preferred_element_type=jnp.float32) * queries.shape[-1] ** -0.5
    positions = jnp.arange(seq_len)
    allowed = (positions[None, :] <= positions[:, None]) & (positions[None, :] < length)
    attn_prob = jax.nn.softmax(jnp.where(allowed, scores, -1e30), axis=-1).astype(jnp.bfloat16)
    return jnp.einsum("kgqs,skh->qkgh", attn_prob, values, preferred_element_type=jnp.float32).astype(jnp.bfloat16)


def gather_rows(row_shard):
    return lax.all_gather(row_shard, "fsdp", axis=0, tiled=True)


def solution(mesh):
    batch_spec = P(("dp", "fsdp"))
    weight_spec = P(None, "fsdp")
    cache_spec = P(None, ("dp", "fsdp"))

    def per_device(hidden_in, lengths, ln_attn_g, ln_attn_b, ln_mlp_g, ln_mlp_b, w_qkv, w_out, w_up, w_down):
        seq_dev, seq_len = hidden_in.shape[0], hidden_in.shape[1]
        group_heads = w_qkv.shape[3] - 2
        cos_full, sin_full = rope_tables(seq_len, w_qkv.shape[4])
        hidden = hidden_in
        key_list = []
        value_list = []
        for layer_idx in range(w_qkv.shape[0]):
            attn_in = layer_norm(hidden, gather_rows(ln_attn_g[layer_idx]), gather_rows(ln_attn_b[layer_idx]))
            mlp_in = layer_norm(hidden, gather_rows(ln_mlp_g[layer_idx]), gather_rows(ln_mlp_b[layer_idx]))
            qkv_full = gather_rows(w_qkv[layer_idx])
            qkv_proj = jnp.einsum("std,dkgh->stkgh", attn_in, qkv_full, preferred_element_type=jnp.float32).astype(jnp.bfloat16)
            queries = rotary(qkv_proj[:, :, :, :group_heads], cos_full[:, None, None, :], sin_full[:, None, None, :])
            key_rot = rotary(qkv_proj[:, :, :, group_heads], cos_full[:, None, :], sin_full[:, None, :])
            values = qkv_proj[:, :, :, group_heads + 1]
            context = lax.map(attend_one, (queries, key_rot, values, lengths)).reshape(seq_dev, seq_len, -1)
            out_full = gather_rows(w_out[layer_idx])
            attn_out = jnp.dot(context, out_full, preferred_element_type=jnp.float32)
            up_full = gather_rows(w_up[layer_idx])
            hidden_mlp = jax.nn.gelu(jnp.dot(mlp_in, up_full, preferred_element_type=jnp.float32), approximate=False).astype(jnp.bfloat16)
            down_full = gather_rows(w_down[layer_idx])
            mlp_out = jnp.dot(hidden_mlp, down_full, preferred_element_type=jnp.float32)
            hidden = (hidden.astype(jnp.float32) + attn_out + mlp_out).astype(jnp.bfloat16)
            key_list.append(jnp.swapaxes(key_rot, 1, 2))
            value_list.append(jnp.swapaxes(values, 1, 2))
        return hidden, jnp.stack(key_list), jnp.stack(value_list)

    return jax.shard_map(per_device, mesh=mesh, in_specs=(batch_spec, batch_spec) + (weight_spec,) * 8, out_specs=(batch_spec, cache_spec, cache_spec), check_vma=False)
```

profile of v0, /device:TPU:0, one launch (start us, length us, event | category | flops | bytes accessed | tf_op | source)
XLA Modules:
  0.0 953.9 jit_solution(14181912850248094030)
XLA Ops:
  7.2 3.0 fusion.334
  10.2 2.1 copy.35
  12.3 0.0 all-gather.27.cloned.1.call-start
  12.4 3.2 fusion.335
  15.6 0.0 all-gather.29.cloned.1.call-start
  15.6 6.0 fusion.332
  21.6 0.0 all-gather.31.cloned.1.call-start
  21.7 6.0 fusion.333
  27.7 0.0 all-gather.33.cloned.1.call-start
  27.8 2.1 copy.38
  29.9 0.0 all-gather.35.cloned.1.call-start
  30.0 0.5 all-gather.35.cloned.1.call-update
  30.6 0.7 all-gather.37.cloned.1.call-update
  31.3 0.0 all-gather.39.cloned.1.call-start
  31.3 0.7 all-gather.39.cloned.1.call-update
  32.7 13.7 %all-gather = f32[1,2048]{1,0:T(1,128)S(1)} all-gather(f32[1,256]{1,0:T(1,128)S(1)} %get-tuple-element.70), channel_id=2, replica_groups=mesh['dp'=1,'fsdp'=8] {'fsdp'}, dimensions={1}, use_global_device_ids=true | all-gather | bytes 9216 | tf_op jit(solution)/shard_map/all_gather | solution.py:45
  46.4 10.8 %all-gather.1 = f32[1,2048]{1,0:T(1,128)S(1)} all-gather(f32[1,256]{1,0:T(1,128)S(1)} %get-tuple-element.72), channel_id=3, replica_groups=mesh['dp'=1,'fsdp'=8] {'fsdp'}, dimensions={1}, use_global_device_ids=true | all-gather | bytes 9216 | tf_op jit(solution)/shard_map/all_gather | solution.py:45
  57.3 10.9 %all-gather.4 = f32[1,2048]{1,0:T(1,128)} all-gather(f32[1,256]{1,0:T(1,128)S(1)} %get-tuple-element.66), channel_id=6, replica_groups=mesh['dp'=1,'fsdp'=8] {'fsdp'}, dimensions={1}, use_global_device_ids=true | all-gather | bytes 9216 | tf_op jit(solution)/shard_map/all_gather | solution.py:45
  68.2 10.9 %all-gather.5 = f32[1,2048]{1,0:T(1,128)} all-gather(f32[1,256]{1,0:T(1,128)S(1)} %get-tuple-element.68), channel_id=7, replica_groups=mesh['dp'=1,'fsdp'=8] {'fsdp'}, dimensions={1}, use_global_device_ids=true | all-gather | bytes 9216 | tf_op jit(solution)/shard_map/all_gather | solution.py:45
  79.0 10.9 %all-gather.8 = f32[1,2048]{1,0:T(1,128)} all-gather(f32[1,256]{1,0:T(1,128)S(1)} %get-tuple-element.69), channel_id=10, replica_groups=mesh['dp'=1,'fsdp'=8] {'fsdp'}, dimensions={1}, use_global_device_ids=true | all-gather | bytes 9216 | tf_op jit(solution)/shard_map/all_gather | solution.py:45
  89.9 10.8 %all-gather.9 = f32[1,2048]{1,0:T(1,128)} all-gather(f32[1,256]{1,0:T(1,128)S(1)} %get-tuple-element.71), channel_id=11, replica_groups=mesh['dp'=1,'fsdp'=8] {'fsdp'}, dimensions={1}, use_global_device_ids=true | all-gather | bytes 9216 | tf_op jit(solution)/shard_map/all_gather | solution.py:45
  100.7 10.8 %all-gather.12 = f32[1,2048]{1,0:T(1,128)S(1)} all-gather(f32[1,256]{1,0:T(1,128)S(1)} %get-tuple-element.65), channel_id=14, replica_groups=mesh['dp'=1,'fsdp'=8] {'fsdp'}, dimensions={1}, use_global_device_ids=true | all-gather | bytes 9216 | tf_op jit(solution)/shard_map/all_gather | solution.py:45
  111.5 11.0 %all-gather.13 = f32[1,2048]{1,0:T(1,128)S(1)} all-gather(f32[1,256]{1,0:T(1,128)S(1)} %get-tuple-element.67), channel_id=15, replica_groups=mesh['dp'=1,'fsdp'=8] {'fsdp'}, dimensions={1}, use_global_device_ids=true | all-gather | bytes 9216 | tf_op jit(solution)/shard_map/all_gather | solution.py:45
  122.5 0.4 fusion.265
  122.9 0.2 convert_reduce_fusion
  123.1 0.4 fusion.181
  123.5 0.7 fusion.263
  124.2 9.3 fusion.191
  133.6 0.9 slice_bitcast_fusion.3
  134.4 0.9 slice_negate_fusion.3
  135.3 0.1 slice_convert_fusion.1
  135.5 0.2 slice_negate_fusion.1
  135.7 0.6 bitcast_select_fusion.1
  136.3 1.2 copy-done.5
  137.5 0.3 fusion.340
  137.8 3.5 fusion.194
  141.3 1.9 copy.23
  143.3 1.5 reshape.459
  144.8 6.0 all-gather.27.cloned.1.call-done
  150.7 6.6 fusion.141
  157.3 150.4 %all-gather.29.cloned.1.call-done = bf16[1,2048,8192]{2,1,0:T(8,128)(2,1)} async-done(((bf16[1,256,8192]{2,1,0:T(8,128)(2,1)}), bf16[1,2048,8192]{2,1,0:T(8,128)(2,1)}) %all-gather.29.cloned.1.call-update) | async-done | bytes 33554448 | tf_op jit(solution)/shard_map/all_gather | solution.py:45
  307.8 156.9 %all-gather.31.cloned.1.call-done = bf16[1,8192,2048]{2,1,0:T(8,128)(2,1)} async-done(((bf16[1,1024,2048]{2,1,0:T(8,128)(2,1)}), bf16[1,8192,2048]{2,1,0:T(8,128)(2,1)}) %all-gather.31.cloned.1.call-update) | async-done | bytes 33554448 | tf_op jit(solution)/shard_map/all_gather | solution.py:45
  464.7 33.1 %fusion.341 = (f32[192]{0:T(256)S(1)}, f32[1,192,2048]{2,1,0:T(8,128)}) fusion(f32[1,192,2048]{2,1,0:T(8,128)} %fusion.141, bf16[1,8192,2048]{2,1,0:T(8,128)(2,1)} %all-gather.31.cloned.1.call-done, bf16[1,2048,8192]{2,1,0:T(8,128)(2,1)} %all-gather.29.cloned.1.call-done, bf16[1,192,2048]{2,1,0:T(8,128)(2,1)S(1)} %copy-done, f32[2048]{0:T(1024)S(1)} %bitcast.255, ...), kind=kOutput, calls=%fused_computation.321 | convolution fusion | flops 12991070208 | bytes 71059712 | tf_op jit(solution)/shard_map/dot_general | solution.py:74
  497.9 1.7 multiply_reduce_fusion
  499.6 50.9 %all-gather.33.cloned.1.call-done = bf16[1,2048,4,4,256]{4,1,3,2,0:T(8,128)(2,1)} async-done(((bf16[1,256,4,4,256]{4,1,3,2,0:T(8,128)(2,1)}), bf16[1,2048,4,4,256]{4,1,3,2,0:T(8,128)(2,1)}) %all-gather.33.cloned.1.call-update) | async-done | bytes 16777232 | tf_op jit(solution)/shard_map/all_gather | solution.py:45
  550.5 9.8 %fusion.188 = bf16[1,192,4,4,256]{4,1,3,2,0:T(8,128)(2,1)S(1)} fusion(bf16[1,2048,4,4,256]{4,1,3,2,0:T(8,128)(2,1)} %all-gather.33.cloned.1.call-done, f32[1,192,2048]{2,1,0:T(8,128)} %get-tuple-element.76, f32[2048]{0:T(1024)S(1)} %bitcast.253, f32[2048]{0:T(1024)S(1)} %bitcast.252, f32[192]{0:T(256)S(1)} %add_rsqrt_fusion, f32[192]{0:T(256)S(1)} %broadcast_multiply_fusion), kind=kOutput, calls=%fused_computation.157 | convolution fusion | flops 3223977984 | bytes 19940864 | tf_op jit(solution)/shard_map/std,dkgh->stkgh/dot_general | solution.py:64
  560.4 0.8 slice_bitcast_fusion.2
  561.2 0.8 slice_negate_fusion.2
  562.1 0.1 slice_convert_fusion
  562.2 0.2 slice_negate_fusion
  562.4 0.7 bitcast_select_fusion
  563.1 1.1 copy-done.4
  564.2 0.3 fusion.346
  564.6 3.5 fusion.195
  568.1 1.9 copy.26
  570.0 1.5 reshape.462
  571.5 1.6 fusion.249
  573.1 0.9 pad_maximum_fusion
  574.0 2.1 pad_maximum_fusion.1
  576.1 24.4 %all-gather.35.cloned.1.call-done = bf16[1,2048,2048]{2,1,0:T(8,128)(2,1)} async-done(((bf16[1,256,2048]{2,1,0:T(8,128)(2,1)}), bf16[1,2048,2048]{2,1,0:T(8,128)(2,1)}) %all-gather.35.cloned.1.call-update) | async-done | bytes 8388624 | tf_op jit(solution)/shard_map/all_gather | solution.py:45
  600.5 5.8 fusion.138
  606.3 151.2 %all-gather.37.cloned.1.call-done = bf16[1,2048,8192]{2,1,0:T(8,128)(2,1)} async-done(((bf16[1,256,8192]{2,1,0:T(8,128)(2,1)}), bf16[1,2048,8192]{2,1,0:T(8,128)(2,1)}) %all-gather.37.cloned.1.call-update) | async-done | bytes 33554448 | tf_op jit(solution)/shard_map/all_gather | solution.py:45
  757.6 157.1 %all-gather.39.cloned.1.call-done = bf16[1,8192,2048]{2,1,0:T(8,128)(2,1)} async-done(((bf16[1,1024,2048]{2,1,0:T(8,128)(2,1)}), bf16[1,8192,2048]{2,1,0:T(8,128)(2,1)}) %all-gather.39.cloned.1.call-update) | async-done | bytes 33554448 | tf_op jit(solution)/shard_map/all_gather | solution.py:45
  914.6 32.4 %fusion.158 = bf16[1,192,2048]{2,1,0:T(8,128)(2,1)} fusion(f32[1,192,2048]{2,1,0:T(8,128)S(1)} %fusion.138, bf16[1,8192,2048]{2,1,0:T(8,128)(2,1)} %all-gather.39.cloned.1.call-done, bf16[1,2048,8192]{2,1,0:T(8,128)(2,1)} %all-gather.37.cloned.1.call-done, f32[1,192,2048]{2,1,0:T(8,128)S(1)} %copy-done.3, f32[2048]{0:T(1024)S(1)} %bitcast.251, ...), kind=kOutput, calls=%fused_computation.126 | convolution fusion | flops 12989890560 | bytes 71058944 | tf_op jit(solution)/shard_map/dot_general | solution.py:74
  (73 shorter events, 0.4 us)
Async XLA Ops:
  7.2 117.0 %all-gather.25.cloned.1.call-start = ((), (), s32[]{:S(2)}) async-start(), calls=%async_computation | async-start | bytes 18874368 | tf_op jit(solution)/shard_map/all_gather | solution.py:45
  12.3 138.4 %all-gather.27.cloned.1.call-start = ((), (), s32[]{:S(2)}) async-start(), calls=%async_computation.1 | async-start | bytes 9437184 | tf_op jit(solution)/shard_map/all_gather | solution.py:45
  15.6 292.2 %all-gather.29.cloned.1.call-start = ((), (), s32[]{:S(2)}) async-start(), calls=%async_computation.2 | async-start | bytes 37748736 | tf_op jit(solution)/shard_map/all_gather | solution.py:45
  21.6 443.1 %all-gather.31.cloned.1.call-start = ((), (), s32[]{:S(2)}) async-start(), calls=%async_computation.3 | async-start | bytes 37748736 | tf_op jit(solution)/shard_map/all_gather | solution.py:45
  27.7 522.8 %all-gather.33.cloned.1.call-start = ((), (), s32[]{:S(2)}) async-start(), calls=%async_computation.4 | async-start | bytes 18874368 | tf_op jit(solution)/shard_map/all_gather | solution.py:45
  29.9 2.8 copy-start.20
  29.9 16.5 %copy-start.21 = (f32[2,256]{1,0:T(2,128)S(1)}, f32[2,256]{1,0:T(2,128)}, u32[]{:S(2)}) copy-start(f32[2,256]{1,0:T(2,128)} %param.13) | copy-start | bytes 6148
  29.9 27.4 %copy-start.22 = (f32[2,256]{1,0:T(2,128)S(1)}, f32[2,256]{1,0:T(2,128)}, u32[]{:S(2)}) copy-start(f32[2,256]{1,0:T(2,128)} %param.14) | copy-start | bytes 6148
  29.9 38.2 %copy-start.23 = (f32[2,256]{1,0:T(2,128)S(1)}, f32[2,256]{1,0:T(2,128)}, u32[]{:S(2)}) copy-start(f32[2,256]{1,0:T(2,128)} %param.15) | copy-start | bytes 6148
  29.9 93.0 %copy-start = (bf16[1,192,2048]{2,1,0:T(8,128)(2,1)S(1)}, bf16[1,192,2048]{2,1,0:T(8,128)(2,1)}, u32[]{:S(2)}) copy-start(bf16[1,192,2048]{2,1,0:T(8,128)(2,1)} %param.10) | copy-start | bytes 2359300
  29.9 570.6 %all-gather.35.cloned.1.call-start = ((), (), s32[]{:S(2)}) async-start(), calls=%async_computation.5 | async-start | bytes 9437184 | tf_op jit(solution)/shard_map/all_gather | solution.py:45
  30.5 727.1 %all-gather.37.cloned.1.call-start = ((), (), s32[]{:S(2)}) async-start(), calls=%async_computation.6 | async-start | bytes 37748736 | tf_op jit(solution)/shard_map/all_gather | solution.py:45
  31.3 883.4 %all-gather.39.cloned.1.call-start = ((), (), s32[]{:S(2)}) async-start(), calls=%async_computation.7 | async-start | bytes 37748736 | tf_op jit(solution)/shard_map/all_gather | solution.py:45
  122.9 12.7 %copy-start.6 = (f32[192,256]{1,0:T(8,128)}, f32[192,256]{1,0:T(8,128)S(1)}, u32[]{:S(2)}) copy-start(f32[192,256]{1,0:T(8,128)S(1)} %get-tuple-element.77) | copy-start | bytes 589828
  122.9 12.7 %copy-start.8 = (f32[192,256]{1,0:T(8,128)}, f32[192,256]{1,0:T(8,128)S(1)}, u32[]{:S(2)}) copy-start(f32[192,256]{1,0:T(8,128)S(1)} %get-tuple-element.78) | copy-start | bytes 589828
  123.1 10.4 %copy-start.18 = (f32[192]{0:T(256)}, f32[192]{0:T(256)S(1)}, u32[]{:S(2)}) copy-start(f32[192]{0:T(256)S(1)} %broadcast_multiply_fusion.1) | copy-start | bytes 2308
  123.5 10.1 %copy-start.26 = (f32[192]{0:T(256)}, f32[192]{0:T(256)S(1)}, u32[]{:S(2)}) copy-start(f32[192]{0:T(256)S(1)} %add_rsqrt_fusion.1) | copy-start | bytes 2308
  133.6 2.1 copy-start.10
  136.3 1.2 copy-start.5
  144.7 319.9 %copy-start.14 = (f32[1,2048]{1,0:T(1,128)S(1)}, f32[1,2048]{1,0:T(1,128)}, u32[]{:S(2)}) copy-start(f32[1,2048]{1,0:T(1,128)} %all-gather.4) | copy-start | bytes 24580
  144.7 319.9 %copy-start.15 = (f32[1,2048]{1,0:T(1,128)S(1)}, f32[1,2048]{1,0:T(1,128)}, u32[]{:S(2)}) copy-start(f32[1,2048]{1,0:T(1,128)} %all-gather.5) | copy-start | bytes 24580
  144.7 319.9 %copy-start.19 = (f32[192]{0:T(256)S(1)}, f32[192]{0:T(256)}, u32[]{:S(2)}) copy-start(f32[192]{0:T(256)} %copy-done.18) | copy-start | bytes 2308
  144.7 319.9 %copy-start.27 = (f32[192]{0:T(256)S(1)}, f32[192]{0:T(256)}, u32[]{:S(2)}) copy-start(f32[192]{0:T(256)} %copy-done.26) | copy-start | bytes 2308
  464.7 85.8 %copy-start.12 = (f32[1,2048]{1,0:T(1,128)S(1)}, f32[1,2048]{1,0:T(1,128)}, u32[]{:S(2)}) copy-start(f32[1,2048]{1,0:T(1,128)} %all-gather.8) | copy-start | bytes 24580
  464.7 85.8 %copy-start.13 = (f32[1,2048]{1,0:T(1,128)S(1)}, f32[1,2048]{1,0:T(1,128)}, u32[]{:S(2)}) copy-start(f32[1,2048]{1,0:T(1,128)} %all-gather.9) | copy-start | bytes 24580
  497.9 52.6 %copy-start.16 = (f32[192]{0:T(256)}, f32[192]{0:T(256)S(1)}, u32[]{:S(2)}) copy-start(f32[192]{0:T(256)S(1)} %broadcast_multiply_fusion) | copy-start | bytes 2308
  499.6 50.9 %copy-start.24 = (f32[192]{0:T(256)}, f32[192]{0:T(256)S(1)}, u32[]{:S(2)}) copy-start(f32[192]{0:T(256)S(1)} %add_rsqrt_fusion) | copy-start | bytes 2308
  560.3 2.8 copy-start.1
  560.3 2.0 copy-start.7
  560.3 2.0 copy-start.9
  560.4 2.0 copy-start.11
  563.1 1.1 copy-start.4
  564.2 7.3 copy-start.2
  576.1 338.6 %copy-start.3 = (f32[1,192,2048]{2,1,0:T(8,128)S(1)}, f32[1,192,2048]{2,1,0:T(8,128)}, u32[]{:S(2)}) copy-start(f32[1,192,2048]{2,1,0:T(8,128)} %get-tuple-element.76) | copy-start | bytes 4718596
  576.1 338.6 %copy-start.17 = (f32[192]{0:T(256)S(1)}, f32[192]{0:T(256)}, u32[]{:S(2)}) copy-start(f32[192]{0:T(256)} %copy-done.16) | copy-start | bytes 2308
  576.1 338.6 %copy-start.25 = (f32[192]{0:T(256)S(1)}, f32[192]{0:T(256)}, u32[]{:S(2)}) copy-start(f32[192]{0:T(256)} %copy-done.24) | copy-start | bytes 2308
Sparse Core Ops, SparseCore 0:
  12.5 87.8 all-gather.24
  102.1 48.5 all-gather.26
  152.5 155.2 all-gather.28
  309.4 155.2 all-gather.30
  466.4 84.0 all-gather.32
  552.1 48.3 all-gather.34
  602.3 155.2 all-gather.36
  759.4 155.2 all-gather.38
where the time goes:
time: 954 us
  waiting for transfers between devices  699 us (73%)
  matrix products  105 us (11%)
  blocking collectives  89.7 us (9%)
  local copies, waits for them, and re-layouts  31.6 us (3%)
  between operations  15.2 us (2%)
  other arithmetic  12.7 us (1%)
    all_gather x8, waiting for transfers between devices, gather_rows(): return lax.all_gather(row_shard, 'fsdp', axis=0, tiled=True)  697 us
    all_gather x8, blocking collectives, gather_rows(): return lax.all_gather(row_shard, 'fsdp', axis=0, tiled=True)  89.7 us
    dot_general x2, matrix products, per_device(): mlp_out = jnp.dot(hidden_mlp, down_full, preferred_element_type=jnp.float32)  65.6 us
    dot_general x2, matrix products, per_device(): jnp.einsum('std,dkgh->stkgh', attn_in, qkv_full, preferred_element_type=j...  19.2 us
  transfers between devices with their start and end apart: 8, of which 7 were waited for; matrix products, arithmetic and copies ran while one was open for 12% of the time, Pallas kernels for 0%

commit v1 on v0

v1 whole, which is shorter than its diff:
```python
import jax
import jax.numpy as jnp
import numpy as np
from jax import lax
from jax.experimental import pallas as pl
from jax.experimental.pallas import tpu as pltpu
from jax.sharding import PartitionSpec as P

MESH = pl.DeviceIdType.MESH
LN_EPS = 1e-5
ROPE_BASE = 10000.0
T = 192
D = 2048
HD = 256
ROWS = 256
QC = 1024
FC = 2048
DR = 1024
CH = 16
TN = 256
F32 = jnp.float32
BF16 = jnp.bfloat16
PACK, QKV0, UP0, QKV1, UP1 = range(5)


def kernel(pack, h_in, wqkv, wout, wup, wdown, cos_ref, sin_ref,
           h_out, kc, vc,
           packg, wq, wu, wo, wd, hg, part, rsb, nb, qkv, ctx, kr, vr, mid,
           ici_s, ici_r, d2d_s, d2d_r, loc, own_s, own_r, own_l,
           h_s, h_r, h_l, rs_s, rs_r, kv_s, kv_r, kv_l, out_l):
    me = lax.axis_index("fsdp")
    core = me % 2
    chip = me // 2
    partner = chip * 2 + (1 - core)

    def chip_at(s):
        return ((chip // 2 + s // 2) % 2) * 2 + (chip % 2 + s % 2) % 2

    def peer(s):
        return chip_at(s) * 2 + core

    def remote(src, dst, send, recv, device):
        return pltpu.make_async_remote_copy(
            src_ref=src, dst_ref=dst, send_sem=send, recv_sem=recv,
            device_id={"fsdp": device}, device_id_type=MESH)

    def cols(c, width):
        return pl.ds(pl.multiple_of(c * width, width), width)

    def source(kind, c):
        if kind == PACK:
            return pack
        if kind in (QKV0, QKV1):
            return wqkv.at[int(kind == QKV1), :, cols(c, QC)]
        return wup.at[int(kind == UP1), :, cols(c, FC)]

    def landing(kind, row):
        if kind == PACK:
            return packg.at[:, cols(row, ROWS)]
        if kind in (QKV0, QKV1):
            return wq.at[int(kind == QKV1), cols(row, ROWS), :]
        return wu.at[int(kind == UP1), cols(row, ROWS), :]

    def ici(kind, s):
        return remote(source(kind, chip_at(s)), landing(kind, me), ici_s.at[kind, s], ici_r.at[kind, s], peer(s))

    def ici_in(kind, s):
        return remote(source(kind, chip), landing(kind, peer(s)), ici_s.at[kind, s], ici_r.at[kind, s], peer(s))

    def d2d(kind, s):
        src = source(kind, chip) if s == 0 else landing(kind, peer(s))
        row = me if s == 0 else peer(s)
        return remote(src, landing(kind, row), d2d_s.at[kind, s], d2d_r.at[kind, s], partner)

    def d2d_in(kind, s):
        row = chip_at(s) * 2 + (1 - core)
        return remote(landing(kind, row), landing(kind, row), d2d_s.at[kind, s], d2d_r.at[kind, s], partner)

    def local(kind):
        return pltpu.make_async_copy(source(kind, chip), landing(kind, me), loc.at[kind])

    def own_refs(layer, which, core_index):
        if which == 0:
            return wout.at[layer], wo.at[layer, cols(core_index, ROWS), :]
        return wdown.at[layer], wd.at[layer, cols(core_index, DR), :]

    def own_remote(layer, which, core_index):
        src, dst = own_refs(layer, which, core_index)
        return remote(src, dst, own_s.at[layer, which], own_r.at[layer, which], partner)

    def own_local(layer, which):
        src, dst = own_refs(layer, which, core)
        return pltpu.make_async_copy(src, dst, own_l.at[layer, which])

    def send_block(kind):
        for s in (3, 1, 2):
            ici(kind, s).start()

    def own_block(kind):
        local(kind).start()
        d2d(kind, 0).start()

    def own_rows(layer):
        for which in range(2):
            own_local(layer, which).start()
            own_remote(layer, which, core).start()

    def relay_block(kind):
        for s in (3, 1, 2):
            ici_in(kind, s).wait_recv()
            d2d(kind, s).start()

    def block_ready(kind):
        local(kind).wait()
        for s in range(4):
            d2d_in(kind, s).wait_recv()

    def own_ready(layer):
        for which in range(2):
            own_local(layer, which).wait()
            own_remote(layer, which, 1 - core).wait_recv()

    def h_copy(layer, s):
        src = h_in if layer == 0 else hg.at[chip]
        return remote(src, hg.at[chip], h_s.at[layer, s], h_r.at[layer, s], peer(s))

    def h_copy_in(layer, s):
        return remote(hg.at[chip_at(s)], hg.at[chip_at(s)], h_s.at[layer, s], h_r.at[layer, s], peer(s))

    def rs_copy(layer, s):
        return remote(part.at[chip_at(s)], rsb.at[s - 1], rs_s.at[layer, s], rs_r.at[layer, s], peer(s))

    def kv_copy(layer, which, s):
        src = (kr, vr)[which].at[chip_at(s)]
        dst = (kc, vc)[which].at[layer, chip]
        return remote(src, dst, kv_s.at[layer, which, s], kv_r.at[layer, which, s], peer(s))

    def kv_copy_in(layer, which, s):
        dst = (kc, vc)[which].at[layer, chip_at(s)]
        return remote(dst, dst, kv_s.at[layer, which, s], kv_r.at[layer, which, s], peer(s))

    def kv_local(layer, which):
        return pltpu.make_async_copy((kr, vr)[which].at[chip], (kc, vc)[which].at[layer, chip], kv_l.at[layer, which])

    def kv_send(layer):
        for which in range(2):
            kv_local(layer, which).start()
            for s in (3, 1, 2):
                kv_copy(layer, which, s).start()

    def kv_sent(layer):
        for which in range(2):
            kv_local(layer, which).wait()
            for s in (3, 1, 2):
                kv_copy(layer, which, s).wait_send()

    def norm(j, gain_row):
        gain = packg[gain_row:gain_row + 1, :]
        bias = packg[gain_row + 2:gain_row + 3, :]

        def step(i, carry):
            rows = pl.ds(pl.multiple_of(i * CH, CH), CH)
            x = hg[j, rows, :].astype(F32)
            mean = jnp.sum(x, axis=-1, keepdims=True) * (1.0 / D)
            x = x - mean
            var = jnp.sum(x * x, axis=-1, keepdims=True) * (1.0 / D)
            nb[rows, :] = (x * lax.rsqrt(var + LN_EPS) * gain + bias).astype(BF16)
            return carry

        lax.fori_loop(0, T // CH, step, 0)

    def rope(u):
        u = u.astype(F32)
        lo, hi = u[:, :HD // 2], u[:, HD // 2:]
        cos, sin = cos_ref[...], sin_ref[...]
        return jnp.concatenate([lo * cos - hi * sin, hi * cos + lo * sin], axis=-1).astype(BF16)

    def attention(layer, j):
        norm(j, layer)

        def project(i, carry):
            n = cols(i, TN)
            qkv[:, n] = jnp.dot(nb[...], wq[layer, :, n], preferred_element_type=F32).astype(BF16)
            return carry

        lax.fori_loop(0, QC // TN, project, 0)
        key = rope(qkv[:, 2 * HD:3 * HD])
        kr[j] = key
        vr[j] = qkv[:, 3 * HD:4 * HD]
        length = packg[8:9, pl.ds(pl.multiple_of((j * 2 + core) * ROWS, ROWS), 128)][:, 0:1]
        query_pos = lax.broadcasted_iota(jnp.int32, (T, T), 0)
        key_pos = lax.broadcasted_iota(jnp.int32, (T, T), 1)
        allowed = (key_pos <= query_pos) & (key_pos.astype(F32) < length)
        for head in range(2):
            query = rope(qkv[:, head * HD:(head + 1) * HD])
            scores = lax.dot_general(query, key, (((1,), (1,)), ((), ())), preferred_element_type=F32) * (HD ** -0.5)
            scores = jnp.where(allowed, scores, -1e30)
            expo = jnp.exp(scores - jnp.max(scores, axis=-1, keepdims=True))
            prob = (expo / jnp.sum(expo, axis=-1, keepdims=True)).astype(BF16)
            ctx[j, :, head * HD:(head + 1) * HD] = jnp.dot(prob, vr[j], preferred_element_type=F32).astype(BF16)

    def mlp(layer, j):
        norm(j, 4 + layer)

        def up(i, carry):
            n = cols(i, TN)
            u = jnp.dot(nb[...], wu[layer, :, n], preferred_element_type=F32)
            mid[:, n] = (0.5 * u * (1.0 + lax.erf(u * np.float32(np.sqrt(0.5))))).astype(BF16)
            return carry

        lax.fori_loop(0, FC // TN, up, 0)

        def down(i, carry):
            n = cols(i, TN)
            acc = jnp.dot(mid[...], wd[layer, :, n], preferred_element_type=F32)
            part[j, :, n] = acc + jnp.dot(ctx[j], wo[layer, :, n], preferred_element_type=F32)
            return carry

        lax.fori_loop(0, D // TN, down, 0)

    def residual(layer):
        for s in (3, 1, 2):
            rs_copy(layer, s).wait_recv()

        def step(i, carry):
            rows = pl.ds(pl.multiple_of(i * CH, CH), CH)
            total = hg[chip, rows, :].astype(F32) + part[chip, rows, :]
            total = total + rsb[0, rows, :] + rsb[1, rows, :] + rsb[2, rows, :]
            hg[chip, rows, :] = total.astype(BF16)
            return carry

        lax.fori_loop(0, T // CH, step, 0)

    barrier = pltpu.get_barrier_semaphore()
    for s in (1, 2, 3):
        pl.semaphore_signal(barrier, inc=1, device_id={"fsdp": peer(s)}, device_id_type=MESH)
    pl.semaphore_signal(barrier, inc=1, device_id={"fsdp": partner}, device_id_type=MESH)
    pl.semaphore_wait(barrier, 4)

    send_block(PACK)
    own_block(PACK)
    for s in (3, 1, 2):
        h_copy(0, s).start()
    h_local = pltpu.make_async_copy(h_in, hg.at[chip], h_l.at[0])
    h_local.start()
    send_block(QKV0)
    send_block(UP0)
    own_block(QKV0)
    own_block(UP0)
    own_rows(0)

    relay_block(PACK)
    block_ready(PACK)
    h_local.wait()
    for s in (3, 1, 2):
        h_copy_in(0, s).wait_recv()
    relay_block(QKV0)
    block_ready(QKV0)

    def attend_step(s, carry):
        attention(0, chip_at(s))
        return carry

    lax.fori_loop(0, 4, attend_step, 0)
    kv_send(0)
    send_block(QKV1)
    own_block(QKV1)
    own_block(UP1)
    own_rows(1)
    relay_block(UP0)
    block_ready(UP0)
    own_ready(0)

    def mlp_step(i, carry):
        s = 3 - i
        mlp(0, chip_at(s))

        @pl.when(s > 0)
        def _():
            rs_copy(0, s).start()

        return carry

    lax.fori_loop(0, 4, mlp_step, 0)
    send_block(UP1)
    relay_block(QKV1)
    for s in (3, 1, 2):
        h_copy(0, s).wait_send()
    residual(0)
    for s in (3, 1, 2):
        h_copy(1, s).start()
    relay_block(UP1)
    block_ready(QKV1)
    block_ready(UP1)
    own_ready(1)
    kv_sent(0)
    for s in (3, 1, 2):
        rs_copy(0, s).wait_send()

    def layer_step(i, carry):
        s = (4 - i) % 4

        @pl.when(s > 0)
        def _():
            h_copy_in(1, s).wait_recv()

        attention(1, chip_at(s))
        mlp(1, chip_at(s))

        @pl.when(s > 0)
        def _():
            rs_copy(1, s).start()

        return carry

    lax.fori_loop(0, 4, layer_step, 0)
    kv_send(1)
    for s in (3, 1, 2):
        h_copy(1, s).wait_send()
    residual(1)
    final = pltpu.make_async_copy(hg.at[chip], h_out, out_l.at[0])
    final.start()

    for kind in range(5):
        for s in (3, 1, 2):
            ici(kind, s).wait_send()
        for s in range(4):
            d2d(kind, s).wait_send()
    for layer in range(2):
        for which in range(2):
            own_remote(layer, which, core).wait_send()
    for s in (3, 1, 2):
        rs_copy(1, s).wait_send()
    kv_sent(1)
    for layer in range(2):
        for which in range(2):
            for s in (3, 1, 2):
                kv_copy_in(layer, which, s).wait_recv()
    final.wait()


def rope_tables():
    half = HD // 2
    inv_freq = np.float32(ROPE_BASE) ** (np.float32(-2.0) * np.arange(half, dtype=np.float32) / np.float32(HD))
    angles = np.arange(T, dtype=np.float32)[:, None] * inv_freq.astype(np.float32)[None, :]
    return np.cos(angles).astype(np.float32), np.sin(angles).astype(np.float32)


def solution(mesh):
    batch_spec = P(("dp", "fsdp"))
    weight_spec = P(None, "fsdp")
    cache_spec = P(None, ("dp", "fsdp"))
    vmem = pl.BlockSpec(memory_space=pltpu.VMEM)
    hbm = pl.BlockSpec(memory_space=pl.ANY)
    dma = pltpu.SemaphoreType.DMA

    def per_device(hidden_in, lengths, ln_attn_g, ln_attn_b, ln_mlp_g, ln_mlp_b, w_qkv, w_out, w_up, w_down):
        length_rows = jnp.broadcast_to(lengths.astype(F32)[:, None], (8, ROWS))
        pack = jnp.concatenate([ln_attn_g, ln_attn_b, ln_mlp_g, ln_mlp_b, length_rows], axis=0)
        cos, sin = rope_tables()
        call = pl.pallas_call(
            kernel,
            out_shape=(
                jax.ShapeDtypeStruct((T, D), BF16),
                jax.ShapeDtypeStruct((2, 4, T, HD), BF16),
                jax.ShapeDtypeStruct((2, 4, T, HD), BF16),
            ),
            in_specs=[vmem, hbm, hbm, hbm, hbm, hbm, vmem, vmem],
            out_specs=(hbm, hbm, hbm),
            scratch_shapes=[
                pltpu.VMEM((16, D), F32),
                pltpu.VMEM((2, D, QC), BF16),
                pltpu.VMEM((2, D, FC), BF16),
                pltpu.VMEM((2, 2 * ROWS, D), BF16),
                pltpu.VMEM((2, 2 * DR, D), BF16),
                pltpu.VMEM((4, T, D), BF16),
                pltpu.VMEM((4, T, D), F32),
                pltpu.VMEM((3, T, D), F32),
                pltpu.VMEM((T, D), BF16),
                pltpu.VMEM((T, QC), BF16),
                pltpu.VMEM((4, T, 2 * HD), BF16),
                pltpu.VMEM((4, T, HD), BF16),
                pltpu.VMEM((4, T, HD), BF16),
                pltpu.VMEM((T, FC), BF16),
                dma((5, 4)), dma((5, 4)), dma((5, 4)), dma((5, 4)), dma((5,)),
                dma((2, 2)), dma((2, 2)), dma((2, 2)),
                dma((2, 4)), dma((2, 4)), dma((1,)),
                dma((2, 4)), dma((2, 4)),
                dma((2, 2, 4)), dma((2, 2, 4)), dma((2, 2)), dma((1,)),
            ],
            compiler_params=pltpu.CompilerParams(
                collective_id=0, has_side_effects=True, vmem_limit_bytes=67043328),
            name="decoder_layers",
        )
        h_out, kc, vc = call(pack, hidden_in[0], w_qkv.reshape(2, ROWS, 4 * QC), w_out, w_up, w_down, cos, sin)
        return h_out[None], kc[:, None], vc[:, None]

    return jax.shard_map(per_device, mesh=mesh, in_specs=(batch_spec, batch_spec) + (weight_spec,) * 8, out_specs=(batch_spec, cache_spec, cache_spec), check_vma=False)
```

time: 954 us -> 382 us (0.40)
  waiting for transfers between devices: 699 us -> 0 us
  Pallas kernels: 0 us -> 364 us
  matrix products: 105 us -> 0 us
  blocking collectives: 89.7 us -> 0 us
  local copies, waits for them, and re-layouts: 31.6 us -> 15.9 us
  between operations: 15.2 us -> 1.29 us
  other arithmetic: 12.7 us -> 0 us
    all_gather x8 -> x0, waiting for transfers between devices: 697 us -> none  [gather_rows(): return lax.all_gather(row_shard, 'fsdp', axis=0, tiled=True)]
    pallas_call x0 -> x1, Pallas kernels: none -> 364 us  [per_device(): call(pack, hidden_in[0], w_qkv.reshape(2, ROWS, 4 * QC), w_out, w_up, w_d...]
    dot_general x10 -> x0, matrix products: 105 us -> none  [the longest x2 65.6 us: per_device(): mlp_out = jnp.dot(hidden_mlp, down_full, preferred_element_type=jnp.float32)]
    all_gather x8 -> x0, blocking collectives: 89.7 us -> none  [gather_rows(): return lax.all_gather(row_shard, 'fsdp', axis=0, tiled=True)]
    slice x8 -> x0, local copies, waits for them, and re-layouts: 18.2 us -> none  [the longest x1 6.04 us: per_device(): down_full = gather_rows(w_down[layer_idx])]
  transfers between devices with their start and end apart: 8 -> 0, of which waited for: 7 -> 0; matrix products, arithmetic and copies ran while one was open for 12% -> 0% of each run, Pallas kernels for 0% -> 0%
where the time goes in v1:
time: 382 us
  Pallas kernels  364 us (95%)
  local copies, waits for them, and re-layouts  15.9 us (4%)
    pallas_call x1, Pallas kernels, per_device(): call(pack, hidden_in[0], w_qkv.reshape(2, ROWS, 4 * QC), w_out, w_up, w_d...  364 us
    reshape x1, local copies, waits for them, and re-layouts, per_device(): w_qkv.reshape(2, ROWS, 4 * QC)  7.74 us

profile of v1, /device:TPU:0, one launch (start us, length us, event | category | flops | bytes accessed | tf_op | source)
XLA Modules:
  0.0 381.6 jit_solution(14306798951406982251)
XLA Ops:
  1.3 1.9 concatenate.3.pack
  3.2 7.7 %reshape.10.wqkv = bf16[2,256,4096]{2,1,0:T(8,128)(2,1)} reshape(bf16[2,256,4,4,256]{4,3,2,1,0:T(4,128)(2,1)} %param.18) | data formatting | bytes 8388608 | tf_op jit(solution)/shard_map/reshape | solution.py:395
  11.0 364.4 %decoder_layers.1 = (bf16[192,2048]{1,0:T(8,128)(2,1)}, bf16[2,4,192,256]{3,2,1,0:T(8,128)(2,1)}, bf16[2,4,192,256]{3,2,1,0:T(8,128)(2,1)}) custom-call(f32[16,256]{1,0:T(8,128)} %concatenate.3.pack, bf16[192,2048]{1,0:T(8,128)(2,1)} %bitcast.9, bf16[2,256,4096]{2,1,0:T(8,128)(2,1)} %reshape.10.wqkv, bf16[2,256,2048]{2,1,0:T(8,128)(2,1)} %wout.1, ...), custom_call_target="tpu_custom_call" | custom-call | tf_op jit(solution)/shard_map/decoder_layers/pallas_call | solution.py:395
  375.4 2.1 copy.21
  377.5 2.1 copy.22
  379.5 2.1 copy.23
  (1 shorter events, 0.0 us)

commit v2 on v1

--- a/solution.py
+++ b/solution.py
@@ -16,6 +16,7 @@
 QC = 1024
 FC = 2048
 DR = 1024
+HALF = D // 2
 CH = 16
 TN = 256
 F32 = jnp.float32
@@ -25,9 +26,9 @@
 
 def kernel(pack, h_in, wqkv, wout, wup, wdown, cos_ref, sin_ref,
            h_out, kc, vc,
-           packg, wq, wu, wo, wd, hg, part, rsb, nb, qkv, ctx, kr, vr, mid,
+           packg, wq, wu, wo, wd, hg, part, rsd, rsb, nb, qkv, ctx, kr, vr, mid,
            ici_s, ici_r, d2d_s, d2d_r, loc, own_s, own_r, own_l,
-           h_s, h_r, h_l, rs_s, rs_r, kv_s, kv_r, kv_l, out_l):
+           h_s, h_r, hf_s, hf_r, h_l, rs_s, rs_r, kv_s, kv_r, kv_l, out_l):
     me = lax.axis_index("fsdp")
     core = me % 2
     chip = me // 2
@@ -92,8 +93,8 @@
         src, dst = own_refs(layer, which, core)
         return pltpu.make_async_copy(src, dst, own_l.at[layer, which])
 
-    def send_block(kind):
-        for s in (3, 1, 2):
+    def send_block(kind, peers=(3, 1, 2)):
+        for s in peers:
             ici(kind, s).start()
 
     def own_block(kind):
@@ -120,15 +121,65 @@
             own_local(layer, which).wait()
             own_remote(layer, which, 1 - core).wait_recv()
 
-    def h_copy(layer, s):
-        src = h_in if layer == 0 else hg.at[chip]
-        return remote(src, hg.at[chip], h_s.at[layer, s], h_r.at[layer, s], peer(s))
-
-    def h_copy_in(layer, s):
-        return remote(hg.at[chip_at(s)], hg.at[chip_at(s)], h_s.at[layer, s], h_r.at[layer, s], peer(s))
-
-    def rs_copy(layer, s):
-        return remote(part.at[chip_at(s)], rsb.at[s - 1], rs_s.at[layer, s], rs_r.at[layer, s], peer(s))
+    def h_half(j, half):
+        return hg.at[j, :, cols(half, HALF)]
+
+    def h_copy(layer, s, half):
+        src = h_in.at[:, cols(half, HALF)] if layer == 0 else h_half(chip, half)
+        return remote(src, h_half(chip, half), h_s.at[layer, s, half], h_r.at[layer, s, half], peer(s))
+
+    def h_copy_in(layer, s, half):
+        dst = h_half(chip_at(s), half)
+        return remote(dst, dst, h_s.at[layer, s, half], h_r.at[layer, s, half], peer(s))
+
+    def h_forward(layer, half):
+        dst = h_half(chip_at(1 + half), half)
+        return remote(dst, dst, hf_s.at[layer, half], hf_r.at[layer, half], peer(2 - half))
+
+    def h_forward_in(layer, half):
+        dst = h_half(chip_at(3), half)
+        return remote(dst, dst, hf_s.at[layer, half], hf_r.at[layer, half], peer(2 - half))
+
+    def h_send(layer):
+        for s, half in ((1, 0), (2, 1), (1, 1), (2, 0)):
+            h_copy(layer, s, half).start()
+
+    def h_relay(layer):
+        for half in range(2):
+            h_copy_in(layer, 1 + half, half).wait_recv()
+            h_forward(layer, half).start()
+
+    def h_ready(layer):
+        for half in range(2):
+            h_copy_in(layer, 2 - half, half).wait_recv()
+        for half in range(2):
+            h_forward_in(layer, half).wait_recv()
+
+    def h_sent(layer):
+        for half in range(2):
+            for s in (1, 2):
+                h_copy(layer, s, half).wait_send()
+            h_forward(layer, half).wait_send()
+
+    def rs_copy(layer, n):
+        s, half, to, dst = (
+            (3, 0, 1, rsd.at[0]), (3, 1, 2, rsd.at[1]),
+            (1, 0, 1, rsb.at[0]), (2, 1, 2, rsb.at[1]),
+            (2, 0, 2, rsb.at[2]), (1, 1, 1, rsb.at[3]))[n]
+        return remote(part.at[chip_at(s), half], dst, rs_s.at[layer, n], rs_r.at[layer, n], peer(to))
+
+    def rs_pass_on(layer):
+        for half in range(2):
+            s = 2 - half
+            rs_copy(layer, half).wait_recv()
+
+            def step(i, carry):
+                rows = pl.ds(pl.multiple_of(i * CH, CH), CH)
+                part[chip_at(s), half, rows, :] = part[chip_at(s), half, rows, :] + rsd[half, rows, :]
+                return carry
+
+            lax.fori_loop(0, T // CH, step, 0)
+            rs_copy(layer, 4 + half).start()
 
     def kv_copy(layer, which, s):
         src = (kr, vr)[which].at[chip_at(s)]
@@ -213,23 +264,44 @@
         def down(i, carry):
             n = cols(i, TN)
             acc = jnp.dot(mid[...], wd[layer, :, n], preferred_element_type=F32)
-            part[j, :, n] = acc + jnp.dot(ctx[j], wo[layer, :, n], preferred_element_type=F32)
+            acc = acc + jnp.dot(ctx[j], wo[layer, :, n], preferred_element_type=F32)
+            part[j, i // (HALF // TN), :, cols(i % (HALF // TN), TN)] = acc
             return carry
 
         lax.fori_loop(0, D // TN, down, 0)
 
     def residual(layer):
-        for s in (3, 1, 2):
-            rs_copy(layer, s).wait_recv()
+        for n in range(2, 6):
+            rs_copy(layer, n).wait_recv()
 
         def step(i, carry):
             rows = pl.ds(pl.multiple_of(i * CH, CH), CH)
-            total = hg[chip, rows, :].astype(F32) + part[chip, rows, :]
-            total = total + rsb[0, rows, :] + rsb[1, rows, :] + rsb[2, rows, :]
-            hg[chip, rows, :] = total.astype(BF16)
+            for half in range(2):
+                n = cols(half, HALF)
+                total = hg[chip, rows, n].astype(F32) + part[chip, half, rows, :]
+                hg[chip, rows, n] = (total + rsb[half, rows, :] + rsb[2 + half, rows, :]).astype(BF16)
             return carry
 
         lax.fori_loop(0, T // CH, step, 0)
+
+    def attend_all(layer, first):
+        def step(s, carry):
+            attention(layer, chip_at(s))
+            return carry
+
+        lax.fori_loop(first, 4, step, 0)
+
+    def mlp_all(layer):
+        def step(i, carry):
+            s = 3 - i
+            mlp(layer, chip_at(s))
+            for n, at in ((0, 3), (1, 3), (2, 1), (3, 2)):
+                @pl.when(s == at)
+                def _():
+                    rs_copy(layer, n).start()
+            return carry
+
+        lax.fori_loop(0, 4, step, 0)
 
     barrier = pltpu.get_barrier_semaphore()
     for s in (1, 2, 3):
@@ -239,29 +311,22 @@
 
     send_block(PACK)
     own_block(PACK)
-    for s in (3, 1, 2):
-        h_copy(0, s).start()
+    h_send(0)
     h_local = pltpu.make_async_copy(h_in, hg.at[chip], h_l.at[0])
     h_local.start()
     send_block(QKV0)
-    send_block(UP0)
     own_block(QKV0)
     own_block(UP0)
     own_rows(0)
-
     relay_block(PACK)
     block_ready(PACK)
+    h_relay(0)
+    send_block(UP0)
     h_local.wait()
-    for s in (3, 1, 2):
-        h_copy_in(0, s).wait_recv()
+    h_ready(0)
     relay_block(QKV0)
     block_ready(QKV0)
-
-    def attend_step(s, carry):
-        attention(0, chip_at(s))
-        return carry
-
-    lax.fori_loop(0, 4, attend_step, 0)
+    attend_all(0, 0)
     kv_send(0)
     send_block(QKV1)
     own_block(QKV1)
@@ -270,53 +335,29 @@
     relay_block(UP0)
     block_ready(UP0)
     own_ready(0)
-
-    def mlp_step(i, carry):
-        s = 3 - i
-        mlp(0, chip_at(s))
-
-        @pl.when(s > 0)
-        def _():
-            rs_copy(0, s).start()
-
-        return carry
-
-    lax.fori_loop(0, 4, mlp_step, 0)
-    send_block(UP1)
+    h_sent(0)
+    mlp_all(0)
+    rs_pass_on(0)
+    send_block(UP1, (3,))
     relay_block(QKV1)
-    for s in (3, 1, 2):
-        h_copy(0, s).wait_send()
+    block_ready(QKV1)
     residual(0)
-    for s in (3, 1, 2):
-        h_copy(1, s).start()
+    h_send(1)
+    kv_sent(0)
+    attention(1, chip)
+    h_relay(1)
+    send_block(UP1, (1, 2))
+    h_ready(1)
+    attend_all(1, 1)
+    kv_send(1)
     relay_block(UP1)
-    block_ready(QKV1)
     block_ready(UP1)
     own_ready(1)
-    kv_sent(0)
-    for s in (3, 1, 2):
-        rs_copy(0, s).wait_send()
-
-    def layer_step(i, carry):
-        s = (4 - i) % 4
-
-        @pl.when(s > 0)
-        def _():
-            h_copy_in(1, s).wait_recv()
-
-        attention(1, chip_at(s))
-        mlp(1, chip_at(s))
-
-        @pl.when(s > 0)
-        def _():
-            rs_copy(1, s).start()
-
-        return carry
-
-    lax.fori_loop(0, 4, layer_step, 0)
-    kv_send(1)
-    for s in (3, 1, 2):
-        h_copy(1, s).wait_send()
+    for n in range(6):
+        rs_copy(0, n).wait_send()
+    mlp_all(1)
+    rs_pass_on(1)
+    h_sent(1)
     residual(1)
     final = pltpu.make_async_copy(hg.at[chip], h_out, out_l.at[0])
     final.start()
@@ -329,8 +370,8 @@
     for layer in range(2):
         for which in range(2):
             own_remote(layer, which, core).wait_send()
-    for s in (3, 1, 2):
-        rs_copy(1, s).wait_send()
+    for n in range(6):
+        rs_copy(1, n).wait_send()
     kv_sent(1)
     for layer in range(2):
         for which in range(2):
@@ -374,8 +415,9 @@
                 pltpu.VMEM((2, 2 * ROWS, D), BF16),
                 pltpu.VMEM((2, 2 * DR, D), BF16),
                 pltpu.VMEM((4, T, D), BF16),
-                pltpu.VMEM((4, T, D), F32),
-                pltpu.VMEM((3, T, D), F32),
+                pltpu.VMEM((4, 2, T, HALF), F32),
+                pltpu.VMEM((2, T, HALF), F32),
+                pltpu.VMEM((4, T, HALF), F32),
                 pltpu.VMEM((T, D), BF16),
                 pltpu.VMEM((T, QC), BF16),
                 pltpu.VMEM((4, T, 2 * HD), BF16),
@@ -384,8 +426,8 @@
                 pltpu.VMEM((T, FC), BF16),
                 dma((5, 4)), dma((5, 4)), dma((5, 4)), dma((5, 4)), dma((5,)),
                 dma((2, 2)), dma((2, 2)), dma((2, 2)),
-                dma((2, 4)), dma((2, 4)), dma((1,)),
-                dma((2, 4)), dma((2, 4)),
+                dma((2, 3, 2)), dma((2, 3, 2)), dma((2, 2)), dma((2, 2)), dma((1,)),
+                dma((2, 6)), dma((2, 6)),
                 dma((2, 2, 4)), dma((2, 2, 4)), dma((2, 2)), dma((1,)),
             ],
             compiler_params=pltpu.CompilerParams(

time: 382 us -> 341 us (0.89)
  Pallas kernels: 364 us -> 324 us
    pallas_call x1, Pallas kernels: 364 us -> 324 us  [per_device(): call(pack, hidden_in[0], w_qkv.reshape(2, ROWS, 4 * QC), w_out, w_up, w_d...]
where the time goes in v2:
time: 341 us
  Pallas kernels  324 us (95%)
  local copies, waits for them, and re-layouts  15.9 us (5%)
    pallas_call x1, Pallas kernels, per_device(): call(pack, hidden_in[0], w_qkv.reshape(2, ROWS, 4 * QC), w_out, w_up, w_d...  324 us
    reshape x1, local copies, waits for them, and re-layouts, per_device(): w_qkv.reshape(2, ROWS, 4 * QC)  7.74 us

profile of v2, /device:TPU:0, one launch (start us, length us, event | category | flops | bytes accessed | tf_op | source)
XLA Modules:
  0.0 341.0 jit_solution(3409792042452654611)
XLA Ops:
  1.3 1.9 concatenate.3.pack
  3.2 7.7 %reshape.10.wqkv = bf16[2,256,4096]{2,1,0:T(8,128)(2,1)} reshape(bf16[2,256,4,4,256]{4,3,2,1,0:T(4,128)(2,1)} %param.18) | data formatting | bytes 8388608 | tf_op jit(solution)/shard_map/reshape | solution.py:437
  11.0 323.8 %decoder_layers.1 = (bf16[192,2048]{1,0:T(8,128)(2,1)}, bf16[2,4,192,256]{3,2,1,0:T(8,128)(2,1)}, bf16[2,4,192,256]{3,2,1,0:T(8,128)(2,1)}) custom-call(f32[16,256]{1,0:T(8,128)} %concatenate.3.pack, bf16[192,2048]{1,0:T(8,128)(2,1)} %bitcast.9, bf16[2,256,4096]{2,1,0:T(8,128)(2,1)} %reshape.10.wqkv, bf16[2,256,2048]{2,1,0:T(8,128)(2,1)} %wout.1, ...), custom_call_target="tpu_custom_call" | custom-call | tf_op jit(solution)/shard_map/decoder_layers/pallas_call | solution.py:437
  334.8 2.1 copy.21
  336.9 2.1 copy.22
  338.9 2.1 copy.23
  (1 shorter events, 0.0 us)

commit v3 on v2

--- a/solution.py
+++ b/solution.py
@@ -17,6 +17,7 @@
 FC = 2048
 DR = 1024
 HALF = D // 2
+RAW = 32
 CH = 16
 TN = 256
 F32 = jnp.float32
@@ -24,11 +25,11 @@
 PACK, QKV0, UP0, QKV1, UP1 = range(5)
 
 
-def kernel(pack, h_in, wqkv, wout, wup, wdown, cos_ref, sin_ref,
+def kernel(len_ref, ga_ref, ba_ref, gm_ref, bm_ref, h_in, wqkv, wout, wup, wdown, cos_ref, sin_ref,
            h_out, kc, vc,
-           packg, wq, wu, wo, wd, hg, part, rsd, rsb, nb, qkv, ctx, kr, vr, mid,
+           pack, raw, packg, wq, wu, wo, wd, hg, part, rsd, rsb, nb, qkv, ctx, kr, vr, mid,
            ici_s, ici_r, d2d_s, d2d_r, loc, own_s, own_r, own_l,
-           h_s, h_r, hf_s, hf_r, h_l, rs_s, rs_r, kv_s, kv_r, kv_l, out_l):
+           raw_l, h_s, h_r, hf_s, hf_r, h_l, rs_s, rs_r, kv_s, kv_r, kv_l, out_l):
     me = lax.axis_index("fsdp")
     core = me % 2
     chip = me // 2
@@ -52,7 +53,7 @@
         if kind == PACK:
             return pack
         if kind in (QKV0, QKV1):
-            return wqkv.at[int(kind == QKV1), :, cols(c, QC)]
+            return wd.at[1, pl.ds(pl.multiple_of(core * DR + int(kind == QKV1) * 2 * ROWS + (c // 2) * ROWS, ROWS), ROWS), cols(c % 2, QC)]
         return wup.at[int(kind == UP1), :, cols(c, FC)]
 
     def landing(kind, row):
@@ -92,6 +93,30 @@
     def own_local(layer, which):
         src, dst = own_refs(layer, which, core)
         return pltpu.make_async_copy(src, dst, own_l.at[layer, which])
+
+    def raw_copy(layer, n, slot):
+        return pltpu.make_async_copy(wqkv.at[layer, pl.ds(n * RAW, RAW)], raw.at[slot], raw_l.at[slot])
+
+    def flatten_qkv(layer):
+        raw_copy(layer, 0, 0).start()
+
+        def step(n, carry):
+            slot = n % 2
+
+            @pl.when(n + 1 < ROWS // RAW)
+            def _():
+                raw_copy(layer, n + 1, 1 - slot).start()
+
+            raw_copy(layer, n, slot).wait()
+            for group in range(4):
+                first = core * DR + layer * 2 * ROWS + (group // 2) * ROWS
+                rows = pl.ds(pl.multiple_of(first + n * RAW, RAW), RAW)
+                for part_of in range(4):
+                    at = (group % 2) * QC + part_of * HD
+                    wd[1, rows, at:at + HD] = raw[slot, :, group, part_of, :]
+            return carry
+
+        lax.fori_loop(0, ROWS // RAW, step, 0)
 
     def send_block(kind, peers=(3, 1, 2)):
         for s in peers:
@@ -284,6 +309,12 @@
 
         lax.fori_loop(0, T // CH, step, 0)
 
+    def qkv_sent():
+        for kind in (QKV0, QKV1):
+            for s in (3, 1, 2):
+                ici(kind, s).wait_send()
+            d2d(kind, 0).wait_send()
+
     def attend_all(layer, first):
         def step(s, carry):
             attention(layer, chip_at(s))
@@ -309,15 +340,20 @@
     pl.semaphore_signal(barrier, inc=1, device_id={"fsdp": partner}, device_id_type=MESH)
     pl.semaphore_wait(barrier, 4)
 
-    send_block(PACK)
-    own_block(PACK)
     h_send(0)
     h_local = pltpu.make_async_copy(h_in, hg.at[chip], h_l.at[0])
     h_local.start()
+    for n, ref in enumerate((ga_ref, ba_ref, gm_ref, bm_ref)):
+        pack[2 * n:2 * n + 2, :] = ref[...]
+    pack[8:16, :] = jnp.full((8, ROWS), len_ref[0].astype(F32), F32)
+    flatten_qkv(0)
+    send_block(PACK)
+    own_block(PACK)
     send_block(QKV0)
     own_block(QKV0)
     own_block(UP0)
     own_rows(0)
+    flatten_qkv(1)
     relay_block(PACK)
     block_ready(PACK)
     h_relay(0)
@@ -331,7 +367,6 @@
     send_block(QKV1)
     own_block(QKV1)
     own_block(UP1)
-    own_rows(1)
     relay_block(UP0)
     block_ready(UP0)
     own_ready(0)
@@ -343,6 +378,8 @@
     block_ready(QKV1)
     residual(0)
     h_send(1)
+    qkv_sent()
+    own_rows(1)
     kv_sent(0)
     attention(1, chip)
     h_relay(1)
@@ -363,10 +400,13 @@
     final.start()
 
     for kind in range(5):
-        for s in (3, 1, 2):
-            ici(kind, s).wait_send()
         for s in range(4):
-            d2d(kind, s).wait_send()
+            if kind not in (QKV0, QKV1):
+                if s > 0:
+                    ici(kind, s).wait_send()
+                d2d(kind, s).wait_send()
+            elif s > 0:
+                d2d(kind, s).wait_send()
     for layer in range(2):
         for which in range(2):
             own_remote(layer, which, core).wait_send()
@@ -380,6 +420,19 @@
     final.wait()
 
 
+def copy_out(h_in, k_in, v_in, h_out, k_out, v_out, h_buf, k_buf, v_buf, in_sem, out_sem):
+    refs = ((h_in, h_buf, h_out), (k_in, k_buf, k_out), (v_in, v_buf, v_out))
+    reads = [pltpu.make_async_copy(src, buf, in_sem.at[n]) for n, (src, buf, _) in enumerate(refs)]
+    writes = [pltpu.make_async_copy(buf, dst, out_sem.at[n]) for n, (_, buf, dst) in enumerate(refs)]
+    for read in reads:
+        read.start()
+    for read, write in zip(reads, writes):
+        read.wait()
+        write.start()
+    for write in writes:
+        write.wait()
+
+
 def rope_tables():
     half = HD // 2
     inv_freq = np.float32(ROPE_BASE) ** (np.float32(-2.0) * np.arange(half, dtype=np.float32) / np.float32(HD))
@@ -396,8 +449,6 @@
     dma = pltpu.SemaphoreType.DMA
 
     def per_device(hidden_in, lengths, ln_attn_g, ln_attn_b, ln_mlp_g, ln_mlp_b, w_qkv, w_out, w_up, w_down):
-        length_rows = jnp.broadcast_to(lengths.astype(F32)[:, None], (8, ROWS))
-        pack = jnp.concatenate([ln_attn_g, ln_attn_b, ln_mlp_g, ln_mlp_b, length_rows], axis=0)
         cos, sin = rope_tables()
         call = pl.pallas_call(
             kernel,
@@ -406,9 +457,11 @@
                 jax.ShapeDtypeStruct((2, 4, T, HD), BF16),
                 jax.ShapeDtypeStruct((2, 4, T, HD), BF16),
             ),
-            in_specs=[vmem, hbm, hbm, hbm, hbm, hbm, vmem, vmem],
+            in_specs=[pl.BlockSpec(memory_space=pltpu.SMEM)] + [vmem] * 4 + [hbm] * 5 + [vmem] * 2,
             out_specs=(hbm, hbm, hbm),
             scratch_shapes=[
+                pltpu.VMEM((16, ROWS), F32),
+                pltpu.VMEM((2, RAW, 4, 4, HD), BF16),
                 pltpu.VMEM((16, D), F32),
                 pltpu.VMEM((2, D, QC), BF16),
                 pltpu.VMEM((2, D, FC), BF16),
@@ -426,7 +479,7 @@
                 pltpu.VMEM((T, FC), BF16),
                 dma((5, 4)), dma((5, 4)), dma((5, 4)), dma((5, 4)), dma((5,)),
                 dma((2, 2)), dma((2, 2)), dma((2, 2)),
-                dma((2, 3, 2)), dma((2, 3, 2)), dma((2, 2)), dma((2, 2)), dma((1,)),
+                dma((2,)), dma((2, 3, 2)), dma((2, 3, 2)), dma((2, 2)), dma((2, 2)), dma((1,)),
                 dma((2, 6)), dma((2, 6)),
                 dma((2, 2, 4)), dma((2, 2, 4)), dma((2, 2)), dma((1,)),
             ],
@@ -434,7 +487,15 @@
                 collective_id=0, has_side_effects=True, vmem_limit_bytes=67043328),
             name="decoder_layers",
         )
-        h_out, kc, vc = call(pack, hidden_in[0], w_qkv.reshape(2, ROWS, 4 * QC), w_out, w_up, w_down, cos, sin)
+        results = call(lengths, ln_attn_g, ln_attn_b, ln_mlp_g, ln_mlp_b, hidden_in[0], w_qkv, w_out, w_up, w_down, cos, sin)
+        h_out, kc, vc = pl.pallas_call(
+            copy_out,
+            out_shape=tuple(jax.ShapeDtypeStruct(r.shape, r.dtype) for r in results),
+            in_specs=[hbm] * 3,
+            out_specs=(hbm,) * 3,
+            scratch_shapes=[pltpu.VMEM(r.shape, r.dtype) for r in results] + [dma((3,)), dma((3,))],
+            name="copy_out",
+        )(*results)
         return h_out[None], kc[:, None], vc[:, None]
 
     return jax.shard_map(per_device, mesh=mesh, in_specs=(batch_spec, batch_spec) + (weight_spec,) * 8, out_specs=(batch_spec, cache_spec, cache_spec), check_vma=False)

time: 341 us -> 327 us (0.959)
  local copies, waits for them, and re-layouts: 15.9 us -> 0 us
    reshape x1 -> x0, local copies, waits for them, and re-layouts: 7.74 us -> none  [per_device(): w_qkv.reshape(2, ROWS, 4 * QC)]
    unnamed x3 -> x0, local copies, waits for them, and re-layouts: 6.21 us -> none
    pallas_call x1 -> x2, Pallas kernels: 324 us -> 325 us  [the longest x1 323 us: per_device(): call(lengths, ln_attn_g, ln_attn_b, ln_mlp_g, ln_mlp_b, hidden_in[0], w_q...]
where the time goes in v3:
time: 327 us
  Pallas kernels  325 us (99%)
    pallas_call x1, Pallas kernels, per_device(): call(lengths, ln_attn_g, ln_attn_b, ln_mlp_g, ln_mlp_b, hidden_in[0], w_q...  323 us

profile of v3, /device:TPU:0, one launch (start us, length us, event | category | flops | bytes accessed | tf_op | source)
XLA Modules:
  0.0 326.7 jit_solution(17574947848555691974)
XLA Ops:
  1.3 322.9 %decoder_layers.1 = (bf16[192,2048]{1,0:T(8,128)(2,1)}, bf16[2,4,192,256]{3,2,1,0:T(8,128)(2,1)}, bf16[2,4,192,256]{3,2,1,0:T(8,128)(2,1)}) custom-call(s32[1]{0:T(128)S(6)} %copy.17.len_ref, f32[2,256]{1,0:T(2,128)} %ga_ref.1, f32[2,256]{1,0:T(2,128)} %ba_ref.1, f32[2,256]{1,0:T(2,128)} %gm_ref.1, f32[2,256]{1,0:T(2,128)} %bm_ref.1, ...), custom_call_target="tpu_custom_call" | custom-call | tf_op jit(solution)/shard_map/decoder_layers/pallas_call | solution.py:490
  324.2 2.6 copy_out.1

commit v4 on v3

--- a/solution.py
+++ b/solution.py
@@ -17,6 +17,8 @@
 FC = 2048
 DR = 1024
 HALF = D // 2
+OUT = 3
+UNROLL = 2
 RAW = 32
 CH = 16
 TN = 256
@@ -27,7 +29,7 @@
 
 def kernel(len_ref, ga_ref, ba_ref, gm_ref, bm_ref, h_in, wqkv, wout, wup, wdown, cos_ref, sin_ref,
            h_out, kc, vc,
-           pack, raw, packg, wq, wu, wo, wd, hg, part, rsd, rsb, nb, qkv, ctx, kr, vr, mid,
+           pack, raw, packg, wq, wu, wo, wd, hg, part, rsd, rsb, nb, qkv, ctx, kr, vr,
            ici_s, ici_r, d2d_s, d2d_r, loc, own_s, own_r, own_l,
            raw_l, h_s, h_r, hf_s, hf_r, h_l, rs_s, rs_r, kv_s, kv_r, kv_l, out_l):
     me = lax.axis_index("fsdp")
@@ -174,7 +176,12 @@
             h_copy_in(layer, 1 + half, half).wait_recv()
             h_forward(layer, half).start()
 
+    def h_forwarded(layer):
+        for half in range(2):
+            h_forward(layer, half).wait_send()
+
     def h_ready(layer):
+        h_forwarded(layer)
         for half in range(2):
             h_copy_in(layer, 2 - half, half).wait_recv()
         for half in range(2):
@@ -184,7 +191,6 @@
         for half in range(2):
             for s in (1, 2):
                 h_copy(layer, s, half).wait_send()
-            h_forward(layer, half).wait_send()
 
     def rs_copy(layer, n):
         s, half, to, dst = (
@@ -207,7 +213,7 @@
             rs_copy(layer, 4 + half).start()
 
     def kv_copy(layer, which, s):
-        src = (kr, vr)[which].at[chip_at(s)]
+        src = (kr, vr)[which].at[layer, chip_at(s)]
         dst = (kc, vc)[which].at[layer, chip]
         return remote(src, dst, kv_s.at[layer, which, s], kv_r.at[layer, which, s], peer(s))
 
@@ -216,7 +222,7 @@
         return remote(dst, dst, kv_s.at[layer, which, s], kv_r.at[layer, which, s], peer(s))
 
     def kv_local(layer, which):
-        return pltpu.make_async_copy((kr, vr)[which].at[chip], (kc, vc)[which].at[layer, chip], kv_l.at[layer, which])
+        return pltpu.make_async_copy((kr, vr)[which].at[layer, chip], (kc, vc)[which].at[layer, chip], kv_l.at[layer, which])
 
     def kv_send(layer):
         for which in range(2):
@@ -230,20 +236,25 @@
             for s in (3, 1, 2):
                 kv_copy(layer, which, s).wait_send()
 
-    def norm(j, gain_row):
-        gain = packg[gain_row:gain_row + 1, :]
-        bias = packg[gain_row + 2:gain_row + 3, :]
+    def hm_slot(s):
+        own = 1 - (s + 3) // 4
+        return own * 4 + (1 - own) * chip_at(s)
+
+    def norm(layer, s):
+        gain_a, bias_a, gain_m, bias_m = (packg[2 * n + layer:2 * n + layer + 1, :] for n in range(4))
 
         def step(i, carry):
             rows = pl.ds(pl.multiple_of(i * CH, CH), CH)
-            x = hg[j, rows, :].astype(F32)
+            x = hg[chip_at(s), rows, :].astype(F32)
             mean = jnp.sum(x, axis=-1, keepdims=True) * (1.0 / D)
             x = x - mean
             var = jnp.sum(x * x, axis=-1, keepdims=True) * (1.0 / D)
-            nb[rows, :] = (x * lax.rsqrt(var + LN_EPS) * gain + bias).astype(BF16)
-            return carry
-
-        lax.fori_loop(0, T // CH, step, 0)
+            x = x * lax.rsqrt(var + LN_EPS)
+            nb[rows, :] = (x * gain_a + bias_a).astype(BF16)
+            hg[hm_slot(s), rows, :] = (x * gain_m + bias_m).astype(BF16)
+            return carry
+
+        lax.fori_loop(0, T // CH, step, 0, unroll=UNROLL)
 
     def rope(u):
         u = u.astype(F32)
@@ -251,8 +262,9 @@
         cos, sin = cos_ref[...], sin_ref[...]
         return jnp.concatenate([lo * cos - hi * sin, hi * cos + lo * sin], axis=-1).astype(BF16)
 
-    def attention(layer, j):
-        norm(j, layer)
+    def attention(layer, s):
+        j = chip_at(s)
+        norm(layer, s)
 
         def project(i, carry):
             n = cols(i, TN)
@@ -261,8 +273,8 @@
 
         lax.fori_loop(0, QC // TN, project, 0)
         key = rope(qkv[:, 2 * HD:3 * HD])
-        kr[j] = key
-        vr[j] = qkv[:, 3 * HD:4 * HD]
+        kr[layer, j] = key
+        vr[layer, j] = qkv[:, 3 * HD:4 * HD]
         length = packg[8:9, pl.ds(pl.multiple_of((j * 2 + core) * ROWS, ROWS), 128)][:, 0:1]
         query_pos = lax.broadcasted_iota(jnp.int32, (T, T), 0)
         key_pos = lax.broadcasted_iota(jnp.int32, (T, T), 1)
@@ -273,22 +285,23 @@
             scores = jnp.where(allowed, scores, -1e30)
             expo = jnp.exp(scores - jnp.max(scores, axis=-1, keepdims=True))
             prob = (expo / jnp.sum(expo, axis=-1, keepdims=True)).astype(BF16)
-            ctx[j, :, head * HD:(head + 1) * HD] = jnp.dot(prob, vr[j], preferred_element_type=F32).astype(BF16)
-
-    def mlp(layer, j):
-        norm(j, 4 + layer)
+            ctx[j, :, head * HD:(head + 1) * HD] = jnp.dot(prob, vr[layer, j], preferred_element_type=F32).astype(BF16)
+
+    def mlp(layer, s):
+        j = chip_at(s)
+        hm = hg.at[hm_slot(s)]
 
         def up(i, carry):
             n = cols(i, TN)
-            u = jnp.dot(nb[...], wu[layer, :, n], preferred_element_type=F32)
-            mid[:, n] = (0.5 * u * (1.0 + lax.erf(u * np.float32(np.sqrt(0.5))))).astype(BF16)
+            u = jnp.dot(hm[...], wu[layer, :, n], preferred_element_type=F32)
+            nb[:, n] = (0.5 * u * (1.0 + lax.erf(u * np.float32(np.sqrt(0.5))))).astype(BF16)
             return carry
 
         lax.fori_loop(0, FC // TN, up, 0)
 
         def down(i, carry):
             n = cols(i, TN)
-            acc = jnp.dot(mid[...], wd[layer, :, n], preferred_element_type=F32)
+            acc = jnp.dot(nb[...], wd[layer, :, n], preferred_element_type=F32)
             acc = acc + jnp.dot(ctx[j], wo[layer, :, n], preferred_element_type=F32)
             part[j, i // (HALF // TN), :, cols(i % (HALF // TN), TN)] = acc
             return carry
@@ -296,18 +309,34 @@
         lax.fori_loop(0, D // TN, down, 0)
 
     def residual(layer):
-        for n in range(2, 6):
-            rs_copy(layer, n).wait_recv()
+        for half in range(2):
+            rs_copy(layer, 2 + half).wait_recv()
+
+        def direct(i, carry):
+            rows = pl.ds(pl.multiple_of(i * CH, CH), CH)
+            for half in range(2):
+                total = hg[chip, rows, cols(half, HALF)].astype(F32) + part[chip, half, rows, :]
+                part[chip, half, rows, :] = total + rsb[half, rows, :]
+            return carry
+
+        lax.fori_loop(0, T // CH, direct, 0)
+        for half in range(2):
+            rs_copy(layer, 4 + half).wait_recv()
 
         def step(i, carry):
             rows = pl.ds(pl.multiple_of(i * CH, CH), CH)
             for half in range(2):
-                n = cols(half, HALF)
-                total = hg[chip, rows, n].astype(F32) + part[chip, half, rows, :]
-                hg[chip, rows, n] = (total + rsb[half, rows, :] + rsb[2 + half, rows, :]).astype(BF16)
-            return carry
-
-        lax.fori_loop(0, T // CH, step, 0)
+                hg[chip, rows, cols(half, HALF)] = (part[chip, half, rows, :] + rsb[2 + half, rows, :]).astype(BF16)
+            return carry
+
+        for n in range(OUT):
+            lax.fori_loop(n * (T // CH // OUT), (n + 1) * (T // CH // OUT), step, 0)
+            if layer == 1:
+                out_copy(n).start()
+
+    def out_copy(n):
+        rows = pl.ds(n * (T // OUT), T // OUT)
+        return pltpu.make_async_copy(hg.at[chip, rows, :], h_out.at[rows, :], out_l.at[n])
 
     def qkv_sent():
         for kind in (QKV0, QKV1):
@@ -317,7 +346,7 @@
 
     def attend_all(layer, first):
         def step(s, carry):
-            attention(layer, chip_at(s))
+            attention(layer, s)
             return carry
 
         lax.fori_loop(first, 4, step, 0)
@@ -325,7 +354,7 @@
     def mlp_all(layer):
         def step(i, carry):
             s = 3 - i
-            mlp(layer, chip_at(s))
+            mlp(layer, s)
             for n, at in ((0, 3), (1, 3), (2, 1), (3, 2)):
                 @pl.when(s == at)
                 def _():
@@ -363,7 +392,6 @@
     relay_block(QKV0)
     block_ready(QKV0)
     attend_all(0, 0)
-    kv_send(0)
     send_block(QKV1)
     own_block(QKV1)
     own_block(UP1)
@@ -380,10 +408,10 @@
     h_send(1)
     qkv_sent()
     own_rows(1)
-    kv_sent(0)
-    attention(1, chip)
+    attention(1, 0)
     h_relay(1)
     send_block(UP1, (1, 2))
+    kv_send(0)
     h_ready(1)
     attend_all(1, 1)
     kv_send(1)
@@ -396,8 +424,6 @@
     rs_pass_on(1)
     h_sent(1)
     residual(1)
-    final = pltpu.make_async_copy(hg.at[chip], h_out, out_l.at[0])
-    final.start()
 
     for kind in range(5):
         for s in range(4):
@@ -412,12 +438,14 @@
             own_remote(layer, which, core).wait_send()
     for n in range(6):
         rs_copy(1, n).wait_send()
+    kv_sent(0)
     kv_sent(1)
     for layer in range(2):
         for which in range(2):
             for s in (3, 1, 2):
                 kv_copy_in(layer, which, s).wait_recv()
-    final.wait()
+    for n in range(OUT):
+        out_copy(n).wait()
 
 
 def copy_out(h_in, k_in, v_in, h_out, k_out, v_out, h_buf, k_buf, v_buf, in_sem, out_sem):
@@ -467,21 +495,20 @@
                 pltpu.VMEM((2, D, FC), BF16),
                 pltpu.VMEM((2, 2 * ROWS, D), BF16),
                 pltpu.VMEM((2, 2 * DR, D), BF16),
-                pltpu.VMEM((4, T, D), BF16),
+                pltpu.VMEM((5, T, D), BF16),
                 pltpu.VMEM((4, 2, T, HALF), F32),
                 pltpu.VMEM((2, T, HALF), F32),
                 pltpu.VMEM((4, T, HALF), F32),
                 pltpu.VMEM((T, D), BF16),
                 pltpu.VMEM((T, QC), BF16),
                 pltpu.VMEM((4, T, 2 * HD), BF16),
-                pltpu.VMEM((4, T, HD), BF16),
-                pltpu.VMEM((4, T, HD), BF16),
-                pltpu.VMEM((T, FC), BF16),
+                pltpu.VMEM((2, 4, T, HD), BF16),
+                pltpu.VMEM((2, 4, T, HD), BF16),
                 dma((5, 4)), dma((5, 4)), dma((5, 4)), dma((5, 4)), dma((5,)),
                 dma((2, 2)), dma((2, 2)), dma((2, 2)),
                 dma((2,)), dma((2, 3, 2)), dma((2, 3, 2)), dma((2, 2)), dma((2, 2)), dma((1,)),
                 dma((2, 6)), dma((2, 6)),
-                dma((2, 2, 4)), dma((2, 2, 4)), dma((2, 2)), dma((1,)),
+                dma((2, 2, 4)), dma((2, 2, 4)), dma((2, 2)), dma((OUT,)),
             ],
             compiler_params=pltpu.CompilerParams(
                 collective_id=0, has_side_effects=True, vmem_limit_bytes=67043328),

time: 327 us -> 319 us (0.976)
  Pallas kernels: 325 us -> 317 us
    pallas_call x1, Pallas kernels: 323 us -> 314 us  [per_device(): call(lengths, ln_attn_g, ln_attn_b, ln_mlp_g, ln_mlp_b, hidden_in[0], w_q...]
where the time goes in v4:
time: 319 us; the launch traced here: 318 us
  Pallas kernels  317 us (99%)
    pallas_call x1, Pallas kernels, per_device(): call(lengths, ln_attn_g, ln_attn_b, ln_mlp_g, ln_mlp_b, hidden_in[0], w_q...  314 us

profile of v4, /device:TPU:0, one launch (start us, length us, event | category | flops | bytes accessed | tf_op | source)
XLA Modules:
  0.0 318.3 jit_solution(3816995853225744465)
XLA Ops:
  1.3 314.4 %decoder_layers.1 = (bf16[192,2048]{1,0:T(8,128)(2,1)}, bf16[2,4,192,256]{3,2,1,0:T(8,128)(2,1)}, bf16[2,4,192,256]{3,2,1,0:T(8,128)(2,1)}) custom-call(s32[1]{0:T(128)S(6)} %copy.17.len_ref, f32[2,256]{1,0:T(2,128)} %ga_ref.1, f32[2,256]{1,0:T(2,128)} %ba_ref.1, f32[2,256]{1,0:T(2,128)} %gm_ref.1, f32[2,256]{1,0:T(2,128)} %bm_ref.1, ...), custom_call_target="tpu_custom_call" | custom-call | tf_op jit(solution)/shard_map/decoder_layers/pallas_call | solution.py:517
  315.7 2.6 copy_out.1

commit v5 on v4

--- a/solution.py
+++ b/solution.py
@@ -17,7 +17,6 @@
 FC = 2048
 DR = 1024
 HALF = D // 2
-OUT = 3
 UNROLL = 2
 RAW = 32
 CH = 16
@@ -27,11 +26,11 @@
 PACK, QKV0, UP0, QKV1, UP1 = range(5)
 
 
-def kernel(len_ref, ga_ref, ba_ref, gm_ref, bm_ref, h_in, wqkv, wout, wup, wdown, cos_ref, sin_ref,
+def kernel(len_ref, ga_ref, ba_ref, gm_ref, bm_ref, h_in, wqkv, wout, wup, wdown, cos_hbm, sin_hbm,
            h_out, kc, vc,
-           pack, raw, packg, wq, wu, wo, wd, hg, part, rsd, rsb, nb, qkv, ctx, kr, vr,
+           cos_ref, sin_ref, pack, raw, packg, wq, wu, wo, wd, hg, part, rsd, rsb, nb, qkv, ctx, kr, vr,
            ici_s, ici_r, d2d_s, d2d_r, loc, own_s, own_r, own_l,
-           raw_l, h_s, h_r, hf_s, hf_r, h_l, rs_s, rs_r, kv_s, kv_r, kv_l, out_l):
+           raw_l, h_s, h_r, hf_s, hf_r, h_l, rs_s, rs_r, kv_s, kv_r, kv_l, const_l, free):
     me = lax.axis_index("fsdp")
     core = me % 2
     chip = me // 2
@@ -62,7 +61,7 @@
         if kind == PACK:
             return packg.at[:, cols(row, ROWS)]
         if kind in (QKV0, QKV1):
-            return wq.at[int(kind == QKV1), cols(row, ROWS), :]
+            return wq.at[cols(row, ROWS), :]
         return wu.at[int(kind == UP1), cols(row, ROWS), :]
 
     def ici(kind, s):
@@ -268,7 +267,7 @@
 
         def project(i, carry):
             n = cols(i, TN)
-            qkv[:, n] = jnp.dot(nb[...], wq[layer, :, n], preferred_element_type=F32).astype(BF16)
+            qkv[:, n] = jnp.dot(nb[...], wq[:, n], preferred_element_type=F32).astype(BF16)
             return carry
 
         lax.fori_loop(0, QC // TN, project, 0)
@@ -326,23 +325,20 @@
         def step(i, carry):
             rows = pl.ds(pl.multiple_of(i * CH, CH), CH)
             for half in range(2):
-                hg[chip, rows, cols(half, HALF)] = (part[chip, half, rows, :] + rsb[2 + half, rows, :]).astype(BF16)
-            return carry
-
-        for n in range(OUT):
-            lax.fori_loop(n * (T // CH // OUT), (n + 1) * (T // CH // OUT), step, 0)
-            if layer == 1:
-                out_copy(n).start()
-
-    def out_copy(n):
-        rows = pl.ds(n * (T // OUT), T // OUT)
-        return pltpu.make_async_copy(hg.at[chip, rows, :], h_out.at[rows, :], out_l.at[n])
+                total = (part[chip, half, rows, :] + rsb[2 + half, rows, :]).astype(BF16)
+                if layer == 0:
+                    hg[chip, rows, cols(half, HALF)] = total
+                else:
+                    h_out[rows, half * HALF:(half + 1) * HALF] = total
+            return carry
+
+        lax.fori_loop(0, T // CH, step, 0)
 
     def qkv_sent():
         for kind in (QKV0, QKV1):
             for s in (3, 1, 2):
                 ici(kind, s).wait_send()
-            d2d(kind, 0).wait_send()
+        d2d(QKV1, 0).wait_send()
 
     def attend_all(layer, first):
         def step(s, carry):
@@ -372,6 +368,10 @@
     h_send(0)
     h_local = pltpu.make_async_copy(h_in, hg.at[chip], h_l.at[0])
     h_local.start()
+    tables = [pltpu.make_async_copy(src, dst, const_l.at[n])
+              for n, (src, dst) in enumerate(((cos_hbm, cos_ref), (sin_hbm, sin_ref)))]
+    for table in tables:
+        table.start()
     for n, ref in enumerate((ga_ref, ba_ref, gm_ref, bm_ref)):
         pack[2 * n:2 * n + 2, :] = ref[...]
     pack[8:16, :] = jnp.full((8, ROWS), len_ref[0].astype(F32), F32)
@@ -388,10 +388,17 @@
     h_relay(0)
     send_block(UP0)
     h_local.wait()
+    for table in tables:
+        table.wait()
     h_ready(0)
     relay_block(QKV0)
     block_ready(QKV0)
     attend_all(0, 0)
+    for s in range(4):
+        d2d(QKV0, s).wait_send()
+    for device in (peer(1), peer(2), peer(3), partner):
+        pl.semaphore_signal(free, inc=1, device_id={"fsdp": device}, device_id_type=MESH)
+    pl.semaphore_wait(free, 4)
     send_block(QKV1)
     own_block(QKV1)
     own_block(UP1)
@@ -431,7 +438,7 @@
                 if s > 0:
                     ici(kind, s).wait_send()
                 d2d(kind, s).wait_send()
-            elif s > 0:
+            elif kind == QKV1 and s > 0:
                 d2d(kind, s).wait_send()
     for layer in range(2):
         for which in range(2):
@@ -444,18 +451,12 @@
         for which in range(2):
             for s in (3, 1, 2):
                 kv_copy_in(layer, which, s).wait_recv()
-    for n in range(OUT):
-        out_copy(n).wait()
-
-
-def copy_out(h_in, k_in, v_in, h_out, k_out, v_out, h_buf, k_buf, v_buf, in_sem, out_sem):
-    refs = ((h_in, h_buf, h_out), (k_in, k_buf, k_out), (v_in, v_buf, v_out))
-    reads = [pltpu.make_async_copy(src, buf, in_sem.at[n]) for n, (src, buf, _) in enumerate(refs)]
-    writes = [pltpu.make_async_copy(buf, dst, out_sem.at[n]) for n, (_, buf, dst) in enumerate(refs)]
-    for read in reads:
-        read.start()
-    for read, write in zip(reads, writes):
-        read.wait()
+
+
+def copy_out(h_in, k_in, v_in, h_out, k_out, v_out, sem):
+    pairs = ((h_in, h_out), (k_in, k_out), (v_in, v_out))
+    writes = [pltpu.make_async_copy(src, dst, sem.at[n]) for n, (src, dst) in enumerate(pairs)]
+    for write in writes:
         write.start()
     for write in writes:
         write.wait()
@@ -481,17 +482,19 @@
         call = pl.pallas_call(
             kernel,
             out_shape=(
-                jax.ShapeDtypeStruct((T, D), BF16),
-                jax.ShapeDtypeStruct((2, 4, T, HD), BF16),
-                jax.ShapeDtypeStruct((2, 4, T, HD), BF16),
+                pltpu.VMEM((T, D), BF16),
+                pltpu.VMEM((2, 4, T, HD), BF16),
+                pltpu.VMEM((2, 4, T, HD), BF16),
             ),
-            in_specs=[pl.BlockSpec(memory_space=pltpu.SMEM)] + [vmem] * 4 + [hbm] * 5 + [vmem] * 2,
-            out_specs=(hbm, hbm, hbm),
+            in_specs=[pl.BlockSpec(memory_space=pltpu.SMEM)] + [vmem] * 4 + [hbm] * 7,
+            out_specs=(vmem, vmem, vmem),
             scratch_shapes=[
+                pltpu.VMEM((T, HD // 2), F32),
+                pltpu.VMEM((T, HD // 2), F32),
                 pltpu.VMEM((16, ROWS), F32),
                 pltpu.VMEM((2, RAW, 4, 4, HD), BF16),
                 pltpu.VMEM((16, D), F32),
-                pltpu.VMEM((2, D, QC), BF16),
+                pltpu.VMEM((D, QC), BF16),
                 pltpu.VMEM((2, D, FC), BF16),
                 pltpu.VMEM((2, 2 * ROWS, D), BF16),
                 pltpu.VMEM((2, 2 * DR, D), BF16),
@@ -508,10 +511,11 @@
                 dma((2, 2)), dma((2, 2)), dma((2, 2)),
                 dma((2,)), dma((2, 3, 2)), dma((2, 3, 2)), dma((2, 2)), dma((2, 2)), dma((1,)),
                 dma((2, 6)), dma((2, 6)),
-                dma((2, 2, 4)), dma((2, 2, 4)), dma((2, 2)), dma((OUT,)),
+                dma((2, 2, 4)), dma((2, 2, 4)), dma((2, 2)), dma((2,)),
+                pltpu.SemaphoreType.REGULAR,
             ],
             compiler_params=pltpu.CompilerParams(
-                collective_id=0, has_side_effects=True, vmem_limit_bytes=67043328),
+                collective_id=0, has_side_effects=True, vmem_limit_bytes=64500000),
             name="decoder_layers",
         )
         results = call(lengths, ln_attn_g, ln_attn_b, ln_mlp_g, ln_mlp_b, hidden_in[0], w_qkv, w_out, w_up, w_down, cos, sin)
@@ -520,7 +524,8 @@
             out_shape=tuple(jax.ShapeDtypeStruct(r.shape, r.dtype) for r in results),
             in_specs=[hbm] * 3,
             out_specs=(hbm,) * 3,
-            scratch_shapes=[pltpu.VMEM(r.shape, r.dtype) for r in results] + [dma((3,)), dma((3,))],
+            scratch_shapes=[dma((3,))],
+            compiler_params=pltpu.CompilerParams(vmem_limit_bytes=1 << 20),
             name="copy_out",
         )(*results)
         return h_out[None], kc[:, None], vc[:, None]

time: 319 us -> 320 us (level)
  no operation moved by 1% of the time
where the time goes in v5:
time: 320 us
  Pallas kernels  318 us (99%)
    pallas_call x1, Pallas kernels, per_device(): call(lengths, ln_attn_g, ln_attn_b, ln_mlp_g, ln_mlp_b, hidden_in[0], w_q...  317 us

profile of v5, /device:TPU:0, one launch (start us, length us, event | category | flops | bytes accessed | tf_op | source)
XLA Modules:
  0.0 319.6 jit_solution(17089557360537334654)
XLA Ops:
  1.3 316.9 %decoder_layers.1 = (bf16[192,2048]{1,0:T(8,128)(2,1)S(1)}, bf16[2,4,192,256]{3,2,1,0:T(8,128)(2,1)S(1)}, bf16[2,4,192,256]{3,2,1,0:T(8,128)(2,1)S(1)}) custom-call(s32[1]{0:T(128)S(6)} %copy.17.len_ref, f32[2,256]{1,0:T(2,128)} %ga_ref.1, f32[2,256]{1,0:T(2,128)} %ba_ref.1, f32[2,256]{1,0:T(2,128)} %gm_ref.1, f32[2,256]{1,0:T(2,128)} %bm_ref.1, ...), custom_call_target="tpu_custom_call" | custom-call | tf_op jit(solution)/shard_map/decoder_layers/pallas_call | solution.py:521
  318.2 1.4 copy_out.1

commit v6 on v5

--- a/solution.py
+++ b/solution.py
@@ -132,10 +132,12 @@
             own_local(layer, which).start()
             own_remote(layer, which, core).start()
 
-    def relay_block(kind):
-        for s in (3, 1, 2):
+    def relay_block(kind, then=None):
+        for n, s in enumerate((3, 1, 2)):
             ici_in(kind, s).wait_recv()
             d2d(kind, s).start()
+            if then is not None and n == 0:
+                then()
 
     def block_ready(kind):
         local(kind).wait()
@@ -220,18 +222,14 @@
         dst = (kc, vc)[which].at[layer, chip_at(s)]
         return remote(dst, dst, kv_s.at[layer, which, s], kv_r.at[layer, which, s], peer(s))
 
-    def kv_local(layer, which):
-        return pltpu.make_async_copy((kr, vr)[which].at[layer, chip], (kc, vc)[which].at[layer, chip], kv_l.at[layer, which])
-
-    def kv_send(layer):
-        for which in range(2):
-            kv_local(layer, which).start()
+    def kv_send(layer, parts=(0, 1)):
+        for which in parts:
+            (kc, vc)[which][layer, chip] = (kr, vr)[which][layer, chip]
             for s in (3, 1, 2):
                 kv_copy(layer, which, s).start()
 
     def kv_sent(layer):
         for which in range(2):
-            kv_local(layer, which).wait()
             for s in (3, 1, 2):
                 kv_copy(layer, which, s).wait_send()
 
@@ -305,11 +303,18 @@
             part[j, i // (HALF // TN), :, cols(i % (HALF // TN), TN)] = acc
             return carry
 
-        lax.fori_loop(0, D // TN, down, 0)
+        for half, sends in ((0, ((0, 3), (2, 1))), (1, ((1, 3), (3, 2)))):
+            lax.fori_loop(half * (HALF // TN), (half + 1) * (HALF // TN), down, 0)
+            for n, at in sends:
+                @pl.when(s == at)
+                def _():
+                    rs_copy(layer, n).start()
 
     def residual(layer):
         for half in range(2):
             rs_copy(layer, 2 + half).wait_recv()
+        if layer == 0:
+            kv_send(0, (0,))
 
         def direct(i, carry):
             rows = pl.ds(pl.multiple_of(i * CH, CH), CH)
@@ -349,12 +354,7 @@
 
     def mlp_all(layer):
         def step(i, carry):
-            s = 3 - i
-            mlp(layer, s)
-            for n, at in ((0, 3), (1, 3), (2, 1), (3, 2)):
-                @pl.when(s == at)
-                def _():
-                    rs_copy(layer, n).start()
+            mlp(layer, 3 - i)
             return carry
 
         lax.fori_loop(0, 4, step, 0)
@@ -386,12 +386,11 @@
     relay_block(PACK)
     block_ready(PACK)
     h_relay(0)
-    send_block(UP0)
+    relay_block(QKV0, lambda: send_block(UP0))
     h_local.wait()
     for table in tables:
         table.wait()
     h_ready(0)
-    relay_block(QKV0)
     block_ready(QKV0)
     attend_all(0, 0)
     for s in range(4):
@@ -399,30 +398,32 @@
     for device in (peer(1), peer(2), peer(3), partner):
         pl.semaphore_signal(free, inc=1, device_id={"fsdp": device}, device_id_type=MESH)
     pl.semaphore_wait(free, 4)
-    send_block(QKV1)
     own_block(QKV1)
     own_block(UP1)
-    relay_block(UP0)
+    relay_block(UP0, lambda: send_block(QKV1))
     block_ready(UP0)
     own_ready(0)
-    h_sent(0)
     mlp_all(0)
     rs_pass_on(0)
-    send_block(UP1, (3,))
     relay_block(QKV1)
     block_ready(QKV1)
+    h_sent(0)
     residual(0)
     h_send(1)
     qkv_sent()
     own_rows(1)
     attention(1, 0)
+    send_block(UP1, (3,))
     h_relay(1)
     send_block(UP1, (1, 2))
-    kv_send(0)
     h_ready(1)
     attend_all(1, 1)
-    kv_send(1)
-    relay_block(UP1)
+
+    def rest_of_kv():
+        kv_send(0, (1,))
+        kv_send(1)
+
+    relay_block(UP1, rest_of_kv)
     block_ready(UP1)
     own_ready(1)
     for n in range(6):

time: 320 us -> 315 us (0.984)
  Pallas kernels: 318 us -> 314 us
    pallas_call x1, Pallas kernels: 317 us -> 312 us  [per_device(): call(lengths, ln_attn_g, ln_attn_b, ln_mlp_g, ln_mlp_b, hidden_in[0], w_q...]
where the time goes in v6:
time: 315 us
  Pallas kernels  314 us (100%)
    pallas_call x1, Pallas kernels, per_device(): call(lengths, ln_attn_g, ln_attn_b, ln_mlp_g, ln_mlp_b, hidden_in[0], w_q...  312 us

profile of v6, /device:TPU:0, one launch (start us, length us, event | category | flops | bytes accessed | tf_op | source)
XLA Modules:
  0.0 314.9 jit_solution(3824859479274368095)
XLA Ops:
  1.3 312.2 %decoder_layers.1 = (bf16[192,2048]{1,0:T(8,128)(2,1)S(1)}, bf16[2,4,192,256]{3,2,1,0:T(8,128)(2,1)S(1)}, bf16[2,4,192,256]{3,2,1,0:T(8,128)(2,1)S(1)}) custom-call(s32[1]{0:T(128)S(6)} %copy.17.len_ref, f32[2,256]{1,0:T(2,128)} %ga_ref.1, f32[2,256]{1,0:T(2,128)} %ba_ref.1, f32[2,256]{1,0:T(2,128)} %gm_ref.1, f32[2,256]{1,0:T(2,128)} %bm_ref.1, ...), custom_call_target="tpu_custom_call" | custom-call | tf_op jit(solution)/shard_map/decoder_layers/pallas_call | solution.py:522
  313.5 1.4 copy_out.1

commit v7 on v6

--- a/solution.py
+++ b/solution.py
@@ -26,11 +26,11 @@
 PACK, QKV0, UP0, QKV1, UP1 = range(5)
 
 
-def kernel(len_ref, ga_ref, ba_ref, gm_ref, bm_ref, h_in, wqkv, wout, wup, wdown, cos_hbm, sin_hbm,
+def kernel(len_ref, ga_hbm, ba_hbm, gm_hbm, bm_hbm, h_in, wqkv, wout, wup, wdown, cos_hbm, sin_hbm,
            h_out, kc, vc,
-           cos_ref, sin_ref, pack, raw, packg, wq, wu, wo, wd, hg, part, rsd, rsb, nb, qkv, ctx, kr, vr,
+           vectors, cos_ref, sin_ref, pack, raw, packg, wq, wu, wo, wd, hg, part, rsd, rsb, nb, qkv, ctx, kr, vr,
            ici_s, ici_r, d2d_s, d2d_r, loc, own_s, own_r, own_l,
-           raw_l, h_s, h_r, hf_s, hf_r, h_l, rs_s, rs_r, kv_s, kv_r, kv_l, const_l, free):
+           raw_l, h_s, h_r, hf_s, hf_r, h_l, rs_s, rs_r, kv_s, kv_r, kv_l, const_l, small_l, free):
     me = lax.axis_index("fsdp")
     core = me % 2
     chip = me // 2
@@ -359,6 +359,10 @@
 
         lax.fori_loop(0, 4, step, 0)
 
+    small = [pltpu.make_async_copy(src, vectors.at[n], small_l.at[n])
+             for n, src in enumerate((ga_hbm, ba_hbm, gm_hbm, bm_hbm))]
+    for copy in small:
+        copy.start()
     barrier = pltpu.get_barrier_semaphore()
     for s in (1, 2, 3):
         pl.semaphore_signal(barrier, inc=1, device_id={"fsdp": peer(s)}, device_id_type=MESH)
@@ -372,8 +376,10 @@
               for n, (src, dst) in enumerate(((cos_hbm, cos_ref), (sin_hbm, sin_ref)))]
     for table in tables:
         table.start()
-    for n, ref in enumerate((ga_ref, ba_ref, gm_ref, bm_ref)):
-        pack[2 * n:2 * n + 2, :] = ref[...]
+    for copy in small:
+        copy.wait()
+    for n in range(4):
+        pack[2 * n:2 * n + 2, :] = vectors[n]
     pack[8:16, :] = jnp.full((8, ROWS), len_ref[0].astype(F32), F32)
     flatten_qkv(0)
     send_block(PACK)
@@ -487,9 +493,10 @@
                 pltpu.VMEM((2, 4, T, HD), BF16),
                 pltpu.VMEM((2, 4, T, HD), BF16),
             ),
-            in_specs=[pl.BlockSpec(memory_space=pltpu.SMEM)] + [vmem] * 4 + [hbm] * 7,
+            in_specs=[pl.BlockSpec(memory_space=pltpu.SMEM)] + [hbm] * 11,
             out_specs=(vmem, vmem, vmem),
             scratch_shapes=[
+                pltpu.VMEM((4, 2, ROWS), F32),
                 pltpu.VMEM((T, HD // 2), F32),
                 pltpu.VMEM((T, HD // 2), F32),
                 pltpu.VMEM((16, ROWS), F32),
@@ -513,6 +520,7 @@
                 dma((2,)), dma((2, 3, 2)), dma((2, 3, 2)), dma((2, 2)), dma((2, 2)), dma((1,)),
                 dma((2, 6)), dma((2, 6)),
                 dma((2, 2, 4)), dma((2, 2, 4)), dma((2, 2)), dma((2,)),
+                dma((5,)),
                 pltpu.SemaphoreType.REGULAR,
             ],
             compiler_params=pltpu.CompilerParams(

time: 315 us -> 314 us (level)
  no operation moved by 1% of the time
where the time goes in v7:
time: 314 us
  Pallas kernels  313 us (100%)
    pallas_call x1, Pallas kernels, per_device(): call(lengths, ln_attn_g, ln_attn_b, ln_mlp_g, ln_mlp_b, hidden_in[0], w_q...  311 us

profile of v7, /device:TPU:0, one launch (start us, length us, event | category | flops | bytes accessed | tf_op | source)
XLA Modules:
  0.0 314.0 jit_solution(16345505929111218484)
XLA Ops:
  1.3 311.3 %decoder_layers.1 = (bf16[192,2048]{1,0:T(8,128)(2,1)S(1)}, bf16[2,4,192,256]{3,2,1,0:T(8,128)(2,1)S(1)}, bf16[2,4,192,256]{3,2,1,0:T(8,128)(2,1)S(1)}) custom-call(s32[1]{0:T(128)S(6)} %copy.17.len_ref, f32[2,256]{1,0:T(2,128)} %ga_hbm.1, f32[2,256]{1,0:T(2,128)} %ba_hbm.1, f32[2,256]{1,0:T(2,128)} %gm_hbm.1, f32[2,256]{1,0:T(2,128)} %bm_hbm.1, ...), custom_call_target="tpu_custom_call" | custom-call | tf_op jit(solution)/shard_map/decoder_layers/pallas_call | solution.py:530
  312.6 1.4 copy_out.1

commit v8 on v7

--- a/solution.py
+++ b/solution.py
@@ -18,6 +18,7 @@
 DR = 1024
 HALF = D // 2
 UNROLL = 2
+PW = ROWS + 128
 RAW = 32
 CH = 16
 TN = 256
@@ -28,7 +29,7 @@
 
 def kernel(len_ref, ga_hbm, ba_hbm, gm_hbm, bm_hbm, h_in, wqkv, wout, wup, wdown, cos_hbm, sin_hbm,
            h_out, kc, vc,
-           vectors, cos_ref, sin_ref, pack, raw, packg, wq, wu, wo, wd, hg, part, rsd, rsb, nb, qkv, ctx, kr, vr,
+           vectors, cos_ref, sin_ref, pack, packl, raw, packg, wq, wu, wo, wd, hg, part, rsd, rsb, nb, qkv, ctx, kr, vr,
            ici_s, ici_r, d2d_s, d2d_r, loc, own_s, own_r, own_l,
            raw_l, h_s, h_r, hf_s, hf_r, h_l, rs_s, rs_r, kv_s, kv_r, kv_l, const_l, small_l, free):
     me = lax.axis_index("fsdp")
@@ -59,7 +60,7 @@
 
     def landing(kind, row):
         if kind == PACK:
-            return packg.at[:, cols(row, ROWS)]
+            return packl.at[row]
         if kind in (QKV0, QKV1):
             return wq.at[cols(row, ROWS), :]
         return wu.at[int(kind == UP1), cols(row, ROWS), :]
@@ -272,7 +273,7 @@
         key = rope(qkv[:, 2 * HD:3 * HD])
         kr[layer, j] = key
         vr[layer, j] = qkv[:, 3 * HD:4 * HD]
-        length = packg[8:9, pl.ds(pl.multiple_of((j * 2 + core) * ROWS, ROWS), 128)][:, 0:1]
+        length = packl[j * 2 + core, 0:1, ROWS:PW][:, 0:1]
         query_pos = lax.broadcasted_iota(jnp.int32, (T, T), 0)
         key_pos = lax.broadcasted_iota(jnp.int32, (T, T), 1)
         allowed = (key_pos <= query_pos) & (key_pos.astype(F32) < length)
@@ -379,8 +380,8 @@
     for copy in small:
         copy.wait()
     for n in range(4):
-        pack[2 * n:2 * n + 2, :] = vectors[n]
-    pack[8:16, :] = jnp.full((8, ROWS), len_ref[0].astype(F32), F32)
+        pack[2 * n:2 * n + 2, 0:ROWS] = vectors[n]
+    pack[:, ROWS:PW] = jnp.full((8, PW - ROWS), len_ref[0].astype(F32), F32)
     flatten_qkv(0)
     send_block(PACK)
     own_block(PACK)
@@ -391,6 +392,8 @@
     flatten_qkv(1)
     relay_block(PACK)
     block_ready(PACK)
+    for n in range(8):
+        packg[:, n * ROWS:(n + 1) * ROWS] = packl[n, :, 0:ROWS]
     h_relay(0)
     relay_block(QKV0, lambda: send_block(UP0))
     h_local.wait()
@@ -411,6 +414,7 @@
     own_ready(0)
     mlp_all(0)
     rs_pass_on(0)
+    send_block(UP1, (3,))
     relay_block(QKV1)
     block_ready(QKV1)
     h_sent(0)
@@ -419,7 +423,6 @@
     qkv_sent()
     own_rows(1)
     attention(1, 0)
-    send_block(UP1, (3,))
     h_relay(1)
     send_block(UP1, (1, 2))
     h_ready(1)
@@ -499,9 +502,10 @@
                 pltpu.VMEM((4, 2, ROWS), F32),
                 pltpu.VMEM((T, HD // 2), F32),
                 pltpu.VMEM((T, HD // 2), F32),
-                pltpu.VMEM((16, ROWS), F32),
+                pltpu.VMEM((8, PW), F32),
+                pltpu.VMEM((8, 8, PW), F32),
                 pltpu.VMEM((2, RAW, 4, 4, HD), BF16),
-                pltpu.VMEM((16, D), F32),
+                pltpu.VMEM((8, D), F32),
                 pltpu.VMEM((D, QC), BF16),
                 pltpu.VMEM((2, D, FC), BF16),
                 pltpu.VMEM((2, 2 * ROWS, D), BF16),

time: 314 us -> 314 us (level)
  no operation moved by 1% of the time
where the time goes in v8:
time: 314 us; the launch traced here: 313 us
  Pallas kernels  312 us (99%)
    pallas_call x1, Pallas kernels, per_device(): call(lengths, ln_attn_g, ln_attn_b, ln_mlp_g, ln_mlp_b, hidden_in[0], w_q...  310 us

profile of v8, /device:TPU:0, one launch (start us, length us, event | category | flops | bytes accessed | tf_op | source)
XLA Modules:
  0.0 313.1 jit_solution(2566279646982547689)
XLA Ops:
  1.3 310.4 %decoder_layers.1 = (bf16[192,2048]{1,0:T(8,128)(2,1)S(1)}, bf16[2,4,192,256]{3,2,1,0:T(8,128)(2,1)S(1)}, bf16[2,4,192,256]{3,2,1,0:T(8,128)(2,1)S(1)}) custom-call(s32[1]{0:T(128)S(6)} %copy.17.len_ref, f32[2,256]{1,0:T(2,128)} %ga_hbm.1, f32[2,256]{1,0:T(2,128)} %ba_hbm.1, f32[2,256]{1,0:T(2,128)} %gm_hbm.1, f32[2,256]{1,0:T(2,128)} %bm_hbm.1, ...), custom_call_target="tpu_custom_call" | custom-call | tf_op jit(solution)/shard_map/decoder_layers/pallas_call | solution.py:534
  311.7 1.4 copy_out.1

commit v9 on v8

--- a/solution.py
+++ b/solution.py
@@ -407,9 +407,10 @@
     for device in (peer(1), peer(2), peer(3), partner):
         pl.semaphore_signal(free, inc=1, device_id={"fsdp": device}, device_id_type=MESH)
     pl.semaphore_wait(free, 4)
+    send_block(QKV1)
     own_block(QKV1)
     own_block(UP1)
-    relay_block(UP0, lambda: send_block(QKV1))
+    relay_block(UP0)
     block_ready(UP0)
     own_ready(0)
     mlp_all(0)

time: 314 us -> 314 us (level)
  no operation moved by 1% of the time
where the time goes in v9:
time: 314 us; the launch traced here: 313 us
  Pallas kernels  312 us (99%)
    pallas_call x1, Pallas kernels, per_device(): call(lengths, ln_attn_g, ln_attn_b, ln_mlp_g, ln_mlp_b, hidden_in[0], w_q...  310 us

profile of v9, /device:TPU:0, one launch (start us, length us, event | category | flops | bytes accessed | tf_op | source)
XLA Modules:
  0.0 313.1 jit_solution(10122306082340086027)
XLA Ops:
  1.3 310.4 %decoder_layers.1 = (bf16[192,2048]{1,0:T(8,128)(2,1)S(1)}, bf16[2,4,192,256]{3,2,1,0:T(8,128)(2,1)S(1)}, bf16[2,4,192,256]{3,2,1,0:T(8,128)(2,1)S(1)}) custom-call(s32[1]{0:T(128)S(6)} %copy.17.len_ref, f32[2,256]{1,0:T(2,128)} %ga_hbm.1, f32[2,256]{1,0:T(2,128)} %ba_hbm.1, f32[2,256]{1,0:T(2,128)} %gm_hbm.1, f32[2,256]{1,0:T(2,128)} %bm_hbm.1, ...), custom_call_target="tpu_custom_call" | custom-call | tf_op jit(solution)/shard_map/decoder_layers/pallas_call | solution.py:535
  311.7 1.4 copy_out.1
